TPU v7x, 256 devices: a whole 4x4x8 slice. The times are simulated.
256 devices in a mesh: wave: 32 (over z, y), lev: 8 (over x, core).
Axes of the slice: x: 4, y: 4, z: 8, core: 2. Of those that a mesh axis runs over, the one named last changes fastest.
Arguments:
- spectral: bfloat16 [128, 6, 128, 1280], P('wave', None, 'lev'), may hold values from -0.01171875 to 0.01171875
- legendre: bfloat16 [128, 640, 1280], P('wave'), may hold values from -4 to 4
- wave_ids: int32 [128], replicated, may hold values from 0 to 1279, as said below
- trunc_lengths: int32 [128], replicated, may hold values from 1 to 1280, as said below
- cycle_points: int32 [1280], replicated, may hold values from 20 to 2560, as said below
- grid_coef: float32 [1280, 2560], P('wave'), may hold values from -6 to 6
- cycle_weights: float32 [640], replicated, may hold values from 0.1 to 2
- modes_in: bfloat16 [128, 128], replicated, may hold values from -0.5 to 0.5
- modes_out: bfloat16 [128, 128], replicated, may hold values from -0.5 to 0.5
- depths: float32 [128], replicated, may hold values from 0.05 to 20
Outputs:
- update: bfloat16 [128, 6, 128, 1280], P('wave', None, 'lev')
Inputs may be any that keep to these rules, and one draw needn't show every extreme that they name: `wave_ids`: distinct zonal wavenumbers; one slot holds wavenumber 0. `trunc_lengths`: the length of slot m is at most 1280 minus wave_ids[m] and at least half of that; the slot of wavenumber 0 has length 1280. `cycle_points`: multiples of 4; cycle j and cycle 1280 - 1-j have the same count; cycles near the equator have 2560.
All inputs are finite; a program needn't handle non-finite values.
Results may differ from a plain program's by a relative error of at most 0.011.
Values may be sent and summed in bfloat16 or wider, within the bound.
A program may use at most 128 MiB of HBM per device.

v0:
```python
import jax
import jax.numpy as jnp
from jax import lax
from jax.sharding import PartitionSpec as P

NT = 1280


def trig_rows(wave_ids, cycle_count, lon_max):
    low_len = 64
    high_len = lon_max // low_len
    counts = cycle_count[:, None, None]
    count_float = counts.astype(jnp.float32)
    low_pts = jnp.arange(low_len, dtype=jnp.int32)
    high_pts = jnp.arange(high_len, dtype=jnp.int32) * low_len
    low_phase = wave_ids[None, :, None] * low_pts[None, None, :] % counts
    high_phase = wave_ids[None, :, None] * high_pts[None, None, :] % counts
    low_angle = 2.0 * jnp.pi * low_phase.astype(jnp.float32) / count_float
    high_angle = 2.0 * jnp.pi * high_phase.astype(jnp.float32) / count_float
    cos_low = jnp.cos(low_angle)[:, :, None, :]
    sin_low = jnp.sin(low_angle)[:, :, None, :]
    cos_high = jnp.cos(high_angle)[:, :, :, None]
    sin_high = jnp.sin(high_angle)[:, :, :, None]
    group_size, wave_total = (cycle_count.shape[0], wave_ids.shape[0])
    cosine = (cos_high * cos_low - sin_high * sin_low).reshape(group_size, wave_total, lon_max)
    sine = (sin_high * cos_low + cos_high * sin_low).reshape(group_size, wave_total, lon_max)
    longitude = jnp.arange(lon_max, dtype=jnp.int32)
    live_mask = (longitude[None, None, :] < counts) & (2 * wave_ids[None, :, None] < counts)
    cosine = jnp.where(live_mask, cosine, 0.0)
    sine_part = jnp.where(live_mask, -sine, 0.0)
    return jnp.stack([cosine, sine_part], axis=1).astype(jnp.bfloat16)


def cycle_trip(fourier, wave_ids, cycle_count, coef_rows):
    wave_total, channels, items, group_size = fourier.shape
    fields = channels // 2
    polys = trig_rows(wave_ids, cycle_count, coef_rows.shape[1])
    factor = jnp.where(wave_ids == 0, 1.0, 2.0).astype(jnp.bfloat16)
    weighted = (fourier * factor[:, None, None, None]).reshape(
        wave_total, 2, fields, items, group_size
    )
    grid_vals = jnp.einsum("mrfig,grmk->gfik", weighted, polys, preferred_element_type=jnp.float32)
    tendency = (grid_vals * (coef_rows[:, None, None, :] + jnp.roll(grid_vals, -1, axis=1))).astype(
        jnp.bfloat16
    )
    analysed = jnp.einsum("gfik,grmk->mrfig", tendency, polys, preferred_element_type=jnp.float32)
    analysed = analysed / cycle_count.astype(jnp.float32)
    return analysed.astype(jnp.bfloat16).reshape(wave_total, channels, items, group_size)


def cycle_group_size():
    for candidate in (8, 4, 2):
        return candidate
    return 1


def damping(depths, own_waves, first, span):
    degree = (own_waves[:, None] + first + jnp.arange(span, dtype=jnp.int32)[None, :]).astype(
        jnp.float32
    )
    return 1.0 / (
        1.0
        + depths[None, :, None] * degree[:, None, :] * (degree[:, None, :] + 1.0) / float(NT * NT)
    )


def inverse_legendre(spectral, legendre, own_lengths):
    wave_local, channels, lev_local, spec_len = spectral.shape
    half_lat = legendre.shape[1]
    row_total = channels * lev_local
    block_width = min(256, spec_len)

    def inverse_per_wave(column, result):
        coeffs = spectral[column].reshape(row_total, spec_len)
        polys = legendre[column]
        length = own_lengths[column]
        blocks = (length + block_width - 1) // block_width

        def inverse_per_block(block_no, sums_pair):
            offset = block_no * block_width
            segment = lax.dynamic_slice_in_dim(coeffs, offset, block_width, 1)
            poly_block = lax.dynamic_slice_in_dim(polys, offset, block_width, 1)
            position = offset + jnp.arange(block_width, dtype=jnp.int32)
            segment = jnp.where(position[None, :] < length, segment, jnp.zeros_like(segment))
            even_sum, odd_sum = sums_pair
            even_piece = jnp.where(position[None, :] % 2 == 0, segment, jnp.zeros_like(segment))
            odd_piece = jnp.where(position[None, :] % 2 == 1, segment, jnp.zeros_like(segment))
            contract = (((1,), (1,)), ((), ()))
            even_sum = even_sum + lax.dot_general(
                even_piece, poly_block, contract, preferred_element_type=jnp.float32
            )
            odd_sum = odd_sum + lax.dot_general(
                odd_piece, poly_block, contract, preferred_element_type=jnp.float32
            )
            return (even_sum, odd_sum)

        zeros_init = jnp.zeros((row_total, half_lat), jnp.float32)
        even_sum, odd_sum = lax.fori_loop(0, blocks, inverse_per_block, (zeros_init, zeros_init))
        northern = even_sum + odd_sum
        southern = jnp.flip(even_sum - odd_sum, axis=1)
        joined = jnp.concatenate([northern, southern], axis=1).astype(jnp.bfloat16)
        return result.at[column].set(joined.reshape(channels, lev_local, 2 * half_lat))

    start_value = jnp.zeros((wave_local, channels, lev_local, 2 * half_lat), jnp.bfloat16)
    return lax.fori_loop(0, wave_local, inverse_per_wave, start_value)


def forward_legendre(returned, legendre, own_lengths, cycle_weights):
    wave_local, channels, lev_local, lat_total = returned.shape
    half_lat = legendre.shape[1]
    spec_len = legendre.shape[2]
    row_total = channels * lev_local
    block_width = min(256, spec_len)
    northern = returned[..., :half_lat].astype(jnp.float32)
    southern = jnp.flip(returned[..., half_lat:], axis=3).astype(jnp.float32)
    even_part = (
        (cycle_weights * (northern + southern))
        .astype(jnp.bfloat16)
        .reshape(wave_local, row_total, half_lat)
    )
    odd_part = (
        (cycle_weights * (northern - southern))
        .astype(jnp.bfloat16)
        .reshape(wave_local, row_total, half_lat)
    )

    def forward_per_wave(column, result):
        polys = legendre[column]
        length = own_lengths[column]
        even_rows = even_part[column]
        odd_rows = odd_part[column]
        blocks = (length + block_width - 1) // block_width

        def forward_per_block(block_no, coeffs):
            offset = block_no * block_width
            poly_block = lax.dynamic_slice_in_dim(polys, offset, block_width, 1)
            position = offset + jnp.arange(block_width, dtype=jnp.int32)
            from_even = jnp.dot(even_rows, poly_block, preferred_element_type=jnp.float32)
            from_odd = jnp.dot(odd_rows, poly_block, preferred_element_type=jnp.float32)
            values = jnp.where(position[None, :] % 2 == 0, from_even, from_odd)
            values = jnp.where(position[None, :] < length, values, 0.0).astype(jnp.bfloat16)
            return lax.dynamic_update_slice_in_dim(coeffs, values, offset, 1)

        coeffs = lax.fori_loop(
            0, blocks, forward_per_block, jnp.zeros((row_total, spec_len), jnp.bfloat16)
        )
        return result.at[column].set(coeffs.reshape(channels, lev_local, spec_len))

    start_value = jnp.zeros((wave_local, channels, lev_local, spec_len), jnp.bfloat16)
    return lax.fori_loop(0, wave_local, forward_per_wave, start_value)


def on_device(
    spectral,
    legendre,
    wave_ids,
    trunc_lengths,
    cycle_points,
    grid_coef,
    cycle_weights,
    modes_in,
    modes_out,
    depths,
):
    wave_rank = lax.axis_index("wave")
    lev_rank = lax.axis_index("lev")
    wave_local, channels, lev_local, spec_len = spectral.shape
    own_waves = lax.dynamic_slice_in_dim(wave_ids, wave_rank * wave_local, wave_local)
    own_lengths = lax.dynamic_slice_in_dim(trunc_lengths, wave_rank * wave_local, wave_local)
    fourier = inverse_legendre(spectral, legendre, own_lengths)
    band_block = lax.all_to_all(fourier, "wave", split_axis=3, concat_axis=0, tiled=True)
    wave_total, chan_count, items, band = band_block.shape
    group_size = cycle_group_size()
    groups = band // group_size
    cycle_count = lax.dynamic_slice_in_dim(cycle_points, wave_rank * band, band)
    stacked = jnp.moveaxis(
        band_block.reshape(wave_total, chan_count, items, groups, group_size), 3, 0
    )
    counts = cycle_count.reshape(groups, group_size)
    coefs = grid_coef.reshape(groups, group_size, grid_coef.shape[1])

    def per_group(packed):
        return cycle_trip(packed[0], wave_ids, packed[1], packed[2])

    results = lax.map(per_group, (stacked, counts, coefs))
    analysed = jnp.moveaxis(results, 0, 3).reshape(wave_total, chan_count, items, band)
    returned = lax.all_to_all(analysed, "wave", split_axis=0, concat_axis=3, tiled=True)
    projected = forward_legendre(returned, legendre, own_lengths, cycle_weights)
    mode_vals = jnp.einsum(
        "kl,mcli->mcki",
        modes_in,
        lax.all_gather(projected, "lev", axis=2, tiled=True),
        preferred_element_type=jnp.float32,
    )
    damp = damping(depths, own_waves, 0, spec_len)
    scaled = (mode_vals * damp[:, None, :, :]).astype(jnp.bfloat16)
    own_rows = lax.dynamic_slice_in_dim(modes_out, lev_rank * lev_local, lev_local, 0)
    update = jnp.einsum(
        "lk,mcki->mcli", own_rows, scaled, preferred_element_type=jnp.float32
    ).astype(jnp.bfloat16)
    return update


def solution(mesh):
    placed = (
        P("wave", None, "lev", None),
        P("wave", None, None),
        P(),
        P(),
        P(),
        P("wave", None),
        P(),
        P(),
        P(),
        P(),
    )
    return jax.shard_map(
        on_device,
        mesh=mesh,
        in_specs=placed,
        out_specs=P("wave", None, "lev", None),
        check_vma=False,
    )
```

profile of v0, /device:TPU:1, one launch (start us, length us, event | category | flops | bytes accessed | tf_op | source)
XLA Modules:
  0.0 546.1 jit_solution(12319821283142474968)
XLA Ops:
  7.4 38.6 %while.138 = (s32[]{:T(128)}, bf16[4,6,16,1280]{3,2,1,0:T(8,128)(2,1)S(1)}, s32[4]{0:T(128)S(1)}, bf16[4,6,16,1280]{3,2,1,0:T(8,128)(2,1)}, bf16[4,640,1280]{2,1...) while((s32[]{:T(128)}, ...), condition=%wide.region_4.5_spmd, body=%wide.region_0.4_spmd.sunk | while | flops 63941424 | bytes 8213980 | solution.py:105
  11.3 6.1 %while.142 = (s32[]{:T(128)}, f32[96,640]{1,0:T(8,128)S(1)}, f32[96,640]{1,0:T(8,128)S(1)}, s32[]{:T(128)}, s32[]{:T(128)}, /*index=5*/bf16[96,1280]{1,0:T(8,128...) while((s32[]{:T(128)}, f32[96,640]{1,0:T(8,128)S(1)}, ...), condition=%wide.region_3.3_spmd, body=%wide.region_2.2_spmd.sunk | while | flops 63142660 | bytes 1741735 | solution.py:98
  30.6 2.4 while.142
  39.0 4.9 while.142
  45.9 7.8 %copy.40 = bf16[4,6,16,1280]{2,0,1,3:T(4,128)(2,1)} copy(bf16[4,6,16,1280]{3,2,1,0:T(8,128)(2,1)S(1)} %get-tuple-element.681) | data formatting | bytes 1966080 | tf_op jit(solution)/shard_map/while | solution.py:105
  53.7 10.9 %reshape.620 = bf16[32,2,7680]{2,1,0:T(2,128)(2,1)} reshape(bf16[1280,6,4,16]{3,2,1,0:T(4,128)(2,1)} %bitcast.156) | data formatting | bytes 1966080
  64.6 11.8 %all-to-all-start = ((bf16[32,2,7680]{2,1,0:T(2,128)(2,1)}), bf16[32,2,7680]{2,1,0:T(2,128)(2,1)S(1)}, u32[]{:S(2)}, u32[]{:S(2)}) async-start(bf16[32,2,7680]{2,1,0:T(2,128)(2,1)} %reshape.620), calls=%async_computation | async-start | bytes 1966080 | tf_op jit(solution)/shard_map/all_to_all | solution.py:171
  77.3 24.1 %all-to-all-done = bf16[32,2,7680]{2,1,0:T(2,128)(2,1)S(1)} async-done(((bf16[32,2,7680]{2,1,0:T(2,128)(2,1)}), bf16[32,2,7680]{2,1,0:T(2,128)(2,1)S(1)}, u32[]{:S(2)}, u32[]{:S(2)}) %all-to-all-start) | async-done | bytes 983072 | tf_op jit(solution)/shard_map/all_to_all | solution.py:171
  101.4 7.2 %reshape.621 = bf16[1280,6,4,16]{3,2,1,0:T(4,128)(2,1)} reshape(bf16[32,2,7680]{2,1,0:T(2,128)(2,1)S(1)} %all-to-all-done) | data formatting | bytes 1966080
  108.5 7.9 %copy.41 = bf16[4,6,16,32,40]{2,4,1,0,3:T(8,128)(2,1)} copy(bf16[4,6,16,32,40]{2,0,1,4,3:T(4,128)(2,1)} %bitcast.157) | data formatting | bytes 1966080 | tf_op jit(solution)/shard_map/all_to_all | solution.py:171
  116.5 7.4 %copy.42 = bf16[5,128,6,16,8]{1,4,3,2,0:T(8,128)(2,1)S(1)} copy(bf16[5,128,6,16,8]{3,4,0,2,1:T(8,128)(2,1)} %bitcast.158) | data formatting | bytes 1966080 | tf_op jit(solution)/shard_map/while | solution.py:185
  123.8 255.6 %while.139 = (s32[]{:T(128)}, bf16[5,128,6,16,8]{1,3,2,4,0:T(8,128)(2,1)S(1)}, s32[5,8]{1,0:T(8,128)S(1)}, s32[128]{0:T(128)S(1)}, bf16[5,128,6,16,8]{1,4,3,2,0:...) while((s32[]{:T(128)}, bf16[5,128,6,16,8]{1,3,2,4,0:T(8,128)(2,1)S(1)}, s32[5,8]{1,0:T(8,128)S(1)}, ...), condition=%wide.region_6.7_spmd, body=%wide.region_5.6_spmd.sunk | while | flops 1069632064 | bytes 128194992 | solution.py:185
  124.1 3.5 fusion.116
  130.0 7.0 %multiply_subtract_fusion.2 = (bf16[8,128,40,64]{1,3,2,0:T(8,128)(2,1)}, bf16[8,128,40,64]{1,3,2,0:T(8,128)(2,1)}) fusion(f32[8,128,64]{1,2,0:T(8,128)S(1)} %get-tuple-element.1013, f32[8,128,40]{1,2,0:T(8,128)S(1)} %get-tuple-element.1014, f32[8,128,64]{1,2,0:T(8,128)S(1)} %get-tuple-element.1015, f32[8,128,40]{1,2,0:T(8,128)S(1)} %get-tuple-element.1016), kind=kLoop, calls=%fused_computation.39.clone.1 | loop fusion | flops 23592960 | bytes 11337728 | tf_op jit(solution)/shard_map/while/body/eval_jaxpr/sub | solution.py:25
  136.9 8.0 %copy.61 = bf16[8,1,128,2560]{3,2,1,0:T(8,128)(2,1)} copy(bf16[8,1,128,2560]{2,3,0,1:T(8,128)(2,1)} %bitcast.150) | data formatting | bytes 10485760 | tf_op jit(solution)/shard_map/while/body/eval_jaxpr/sub | solution.py:25
  144.9 8.0 %copy.62 = bf16[8,1,128,2560]{3,2,1,0:T(8,128)(2,1)} copy(bf16[8,1,128,2560]{2,3,0,1:T(8,128)(2,1)} %bitcast.149) | data formatting | bytes 10485760 | tf_op jit(solution)/shard_map/while/body/eval_jaxpr/neg | solution.py:30
  153.1 11.1 %fusion.118 = (bf16[8,1,128,2560]{3,2,1,0:T(8,128)(2,1)}, bf16[8,1,128,2560]{3,2,1,0:T(8,128)(2,1)}) fusion(bf16[8,1,128,2560]{3,2,1,0:T(8,128)(2,1)} %copy.61, pred[8,128]{1,0:T(8,128)(4,1)S(1)} %broadcast_compare_fusion.8, pred[8,2560]{1,0:T(8,128)(4,1)S(1)} %iota_compare_fusion.2, bf16[8,1,128,2560]{3,2,1,0:T(8,128)(2,1)} %copy.62), kind=kLoop, calls=%fused_computation.31.clone.1 | loop fusion | flops 7864320 | bytes 20993024 | tf_op jit(solution)/shard_map/convert
  164.3 5.8 %fusion.120 = f32[8,3,16,2560]{3,2,1,0:T(8,128)S(1)} fusion(bf16[8,1,128,2560]{3,2,1,0:T(8,128)(2,1)} %get-tuple-element.1019, bf16[8,1,128,2560]{3,2,1,0:T(8,128)(2,1)} %get-tuple-element.1020, bf16[128,2,3,16,8]{0,4,3,2,1:T(8,128)(2,1)S(1)} %broadcast_multiply_fusion.8), kind=kOutput, calls=%fused_computation.40.clone.1 | convolution fusion | flops 508559360 | bytes 14614528 | tf_op jit(solution)/shard_map/while/body/eval_jaxpr/mrfig,grmk->gfik/dot_general | solution.py:42
  171.4 3.6 fusion.121
  175.1 3.5 fusion.116
  178.8 2.3 fusion.117
  181.0 7.0 %multiply_subtract_fusion.2 = (bf16[8,128,40,64]{1,3,2,0:T(8,128)(2,1)}, bf16[8,128,40,64]{1,3,2,0:T(8,128)(2,1)}) fusion(f32[8,128,64]{1,2,0:T(8,128)S(1)} %get-tuple-element.1013, f32[8,128,40]{1,2,0:T(8,128)S(1)} %get-tuple-element.1014, f32[8,128,64]{1,2,0:T(8,128)S(1)} %get-tuple-element.1015, f32[8,128,40]{1,2,0:T(8,128)S(1)} %get-tuple-element.1016), kind=kLoop, calls=%fused_computation.39.clone.1 | loop fusion | flops 23592960 | bytes 11337728 | tf_op jit(solution)/shard_map/while/body/eval_jaxpr/sub | solution.py:25
  188.0 8.0 %copy.61 = bf16[8,1,128,2560]{3,2,1,0:T(8,128)(2,1)} copy(bf16[8,1,128,2560]{2,3,0,1:T(8,128)(2,1)} %bitcast.150) | data formatting | bytes 10485760 | tf_op jit(solution)/shard_map/while/body/eval_jaxpr/sub | solution.py:25
  196.0 8.0 %copy.62 = bf16[8,1,128,2560]{3,2,1,0:T(8,128)(2,1)} copy(bf16[8,1,128,2560]{2,3,0,1:T(8,128)(2,1)} %bitcast.149) | data formatting | bytes 10485760 | tf_op jit(solution)/shard_map/while/body/eval_jaxpr/neg | solution.py:30
  204.1 11.1 %fusion.118 = (bf16[8,1,128,2560]{3,2,1,0:T(8,128)(2,1)}, bf16[8,1,128,2560]{3,2,1,0:T(8,128)(2,1)}) fusion(bf16[8,1,128,2560]{3,2,1,0:T(8,128)(2,1)} %copy.61, pred[8,128]{1,0:T(8,128)(4,1)S(1)} %broadcast_compare_fusion.8, pred[8,2560]{1,0:T(8,128)(4,1)S(1)} %iota_compare_fusion.2, bf16[8,1,128,2560]{3,2,1,0:T(8,128)(2,1)} %copy.62), kind=kLoop, calls=%fused_computation.31.clone.1 | loop fusion | flops 7864320 | bytes 20993024 | tf_op jit(solution)/shard_map/convert
  215.3 5.8 %fusion.120 = f32[8,3,16,2560]{3,2,1,0:T(8,128)S(1)} fusion(bf16[8,1,128,2560]{3,2,1,0:T(8,128)(2,1)} %get-tuple-element.1019, bf16[8,1,128,2560]{3,2,1,0:T(8,128)(2,1)} %get-tuple-element.1020, bf16[128,2,3,16,8]{0,4,3,2,1:T(8,128)(2,1)S(1)} %broadcast_multiply_fusion.8), kind=kOutput, calls=%fused_computation.40.clone.1 | convolution fusion | flops 508559360 | bytes 14614528 | tf_op jit(solution)/shard_map/while/body/eval_jaxpr/mrfig,grmk->gfik/dot_general | solution.py:42
  222.4 3.6 fusion.121
  226.2 3.5 fusion.116
  229.8 2.3 fusion.117
  232.0 7.0 %multiply_subtract_fusion.2 = (bf16[8,128,40,64]{1,3,2,0:T(8,128)(2,1)}, bf16[8,128,40,64]{1,3,2,0:T(8,128)(2,1)}) fusion(f32[8,128,64]{1,2,0:T(8,128)S(1)} %get-tuple-element.1013, f32[8,128,40]{1,2,0:T(8,128)S(1)} %get-tuple-element.1014, f32[8,128,64]{1,2,0:T(8,128)S(1)} %get-tuple-element.1015, f32[8,128,40]{1,2,0:T(8,128)S(1)} %get-tuple-element.1016), kind=kLoop, calls=%fused_computation.39.clone.1 | loop fusion | flops 23592960 | bytes 11337728 | tf_op jit(solution)/shard_map/while/body/eval_jaxpr/sub | solution.py:25
  239.0 8.0 %copy.61 = bf16[8,1,128,2560]{3,2,1,0:T(8,128)(2,1)} copy(bf16[8,1,128,2560]{2,3,0,1:T(8,128)(2,1)} %bitcast.150) | data formatting | bytes 10485760 | tf_op jit(solution)/shard_map/while/body/eval_jaxpr/sub | solution.py:25
  247.0 8.0 %copy.62 = bf16[8,1,128,2560]{3,2,1,0:T(8,128)(2,1)} copy(bf16[8,1,128,2560]{2,3,0,1:T(8,128)(2,1)} %bitcast.149) | data formatting | bytes 10485760 | tf_op jit(solution)/shard_map/while/body/eval_jaxpr/neg | solution.py:30
  255.1 11.1 %fusion.118 = (bf16[8,1,128,2560]{3,2,1,0:T(8,128)(2,1)}, bf16[8,1,128,2560]{3,2,1,0:T(8,128)(2,1)}) fusion(bf16[8,1,128,2560]{3,2,1,0:T(8,128)(2,1)} %copy.61, pred[8,128]{1,0:T(8,128)(4,1)S(1)} %broadcast_compare_fusion.8, pred[8,2560]{1,0:T(8,128)(4,1)S(1)} %iota_compare_fusion.2, bf16[8,1,128,2560]{3,2,1,0:T(8,128)(2,1)} %copy.62), kind=kLoop, calls=%fused_computation.31.clone.1 | loop fusion | flops 7864320 | bytes 20993024 | tf_op jit(solution)/shard_map/convert
  266.3 5.8 %fusion.120 = f32[8,3,16,2560]{3,2,1,0:T(8,128)S(1)} fusion(bf16[8,1,128,2560]{3,2,1,0:T(8,128)(2,1)} %get-tuple-element.1019, bf16[8,1,128,2560]{3,2,1,0:T(8,128)(2,1)} %get-tuple-element.1020, bf16[128,2,3,16,8]{0,4,3,2,1:T(8,128)(2,1)S(1)} %broadcast_multiply_fusion.8), kind=kOutput, calls=%fused_computation.40.clone.1 | convolution fusion | flops 508559360 | bytes 14614528 | tf_op jit(solution)/shard_map/while/body/eval_jaxpr/mrfig,grmk->gfik/dot_general | solution.py:42
  273.4 3.6 fusion.121
  277.2 3.5 fusion.116
  280.8 2.3 fusion.117
  283.1 7.0 %multiply_subtract_fusion.2 = (bf16[8,128,40,64]{1,3,2,0:T(8,128)(2,1)}, bf16[8,128,40,64]{1,3,2,0:T(8,128)(2,1)}) fusion(f32[8,128,64]{1,2,0:T(8,128)S(1)} %get-tuple-element.1013, f32[8,128,40]{1,2,0:T(8,128)S(1)} %get-tuple-element.1014, f32[8,128,64]{1,2,0:T(8,128)S(1)} %get-tuple-element.1015, f32[8,128,40]{1,2,0:T(8,128)S(1)} %get-tuple-element.1016), kind=kLoop, calls=%fused_computation.39.clone.1 | loop fusion | flops 23592960 | bytes 11337728 | tf_op jit(solution)/shard_map/while/body/eval_jaxpr/sub | solution.py:25
  290.0 8.0 %copy.61 = bf16[8,1,128,2560]{3,2,1,0:T(8,128)(2,1)} copy(bf16[8,1,128,2560]{2,3,0,1:T(8,128)(2,1)} %bitcast.150) | data formatting | bytes 10485760 | tf_op jit(solution)/shard_map/while/body/eval_jaxpr/sub | solution.py:25
  298.0 8.0 %copy.62 = bf16[8,1,128,2560]{3,2,1,0:T(8,128)(2,1)} copy(bf16[8,1,128,2560]{2,3,0,1:T(8,128)(2,1)} %bitcast.149) | data formatting | bytes 10485760 | tf_op jit(solution)/shard_map/while/body/eval_jaxpr/neg | solution.py:30
  306.2 11.1 %fusion.118 = (bf16[8,1,128,2560]{3,2,1,0:T(8,128)(2,1)}, bf16[8,1,128,2560]{3,2,1,0:T(8,128)(2,1)}) fusion(bf16[8,1,128,2560]{3,2,1,0:T(8,128)(2,1)} %copy.61, pred[8,128]{1,0:T(8,128)(4,1)S(1)} %broadcast_compare_fusion.8, pred[8,2560]{1,0:T(8,128)(4,1)S(1)} %iota_compare_fusion.2, bf16[8,1,128,2560]{3,2,1,0:T(8,128)(2,1)} %copy.62), kind=kLoop, calls=%fused_computation.31.clone.1 | loop fusion | flops 7864320 | bytes 20993024 | tf_op jit(solution)/shard_map/convert
  317.4 5.8 %fusion.120 = f32[8,3,16,2560]{3,2,1,0:T(8,128)S(1)} fusion(bf16[8,1,128,2560]{3,2,1,0:T(8,128)(2,1)} %get-tuple-element.1019, bf16[8,1,128,2560]{3,2,1,0:T(8,128)(2,1)} %get-tuple-element.1020, bf16[128,2,3,16,8]{0,4,3,2,1:T(8,128)(2,1)S(1)} %broadcast_multiply_fusion.8), kind=kOutput, calls=%fused_computation.40.clone.1 | convolution fusion | flops 508559360 | bytes 14614528 | tf_op jit(solution)/shard_map/while/body/eval_jaxpr/mrfig,grmk->gfik/dot_general | solution.py:42
  324.5 3.6 fusion.121
  328.2 3.5 fusion.116
  331.8 2.3 fusion.117
  334.1 7.0 %multiply_subtract_fusion.2 = (bf16[8,128,40,64]{1,3,2,0:T(8,128)(2,1)}, bf16[8,128,40,64]{1,3,2,0:T(8,128)(2,1)}) fusion(f32[8,128,64]{1,2,0:T(8,128)S(1)} %get-tuple-element.1013, f32[8,128,40]{1,2,0:T(8,128)S(1)} %get-tuple-element.1014, f32[8,128,64]{1,2,0:T(8,128)S(1)} %get-tuple-element.1015, f32[8,128,40]{1,2,0:T(8,128)S(1)} %get-tuple-element.1016), kind=kLoop, calls=%fused_computation.39.clone.1 | loop fusion | flops 23592960 | bytes 11337728 | tf_op jit(solution)/shard_map/while/body/eval_jaxpr/sub | solution.py:25
  341.1 8.0 %copy.61 = bf16[8,1,128,2560]{3,2,1,0:T(8,128)(2,1)} copy(bf16[8,1,128,2560]{2,3,0,1:T(8,128)(2,1)} %bitcast.150) | data formatting | bytes 10485760 | tf_op jit(solution)/shard_map/while/body/eval_jaxpr/sub | solution.py:25
  349.1 8.0 %copy.62 = bf16[8,1,128,2560]{3,2,1,0:T(8,128)(2,1)} copy(bf16[8,1,128,2560]{2,3,0,1:T(8,128)(2,1)} %bitcast.149) | data formatting | bytes 10485760 | tf_op jit(solution)/shard_map/while/body/eval_jaxpr/neg | solution.py:30
  357.2 11.1 %fusion.118 = (bf16[8,1,128,2560]{3,2,1,0:T(8,128)(2,1)}, bf16[8,1,128,2560]{3,2,1,0:T(8,128)(2,1)}) fusion(bf16[8,1,128,2560]{3,2,1,0:T(8,128)(2,1)} %copy.61, pred[8,128]{1,0:T(8,128)(4,1)S(1)} %broadcast_compare_fusion.8, pred[8,2560]{1,0:T(8,128)(4,1)S(1)} %iota_compare_fusion.2, bf16[8,1,128,2560]{3,2,1,0:T(8,128)(2,1)} %copy.62), kind=kLoop, calls=%fused_computation.31.clone.1 | loop fusion | flops 7864320 | bytes 20993024 | tf_op jit(solution)/shard_map/convert
  368.4 5.8 %fusion.120 = f32[8,3,16,2560]{3,2,1,0:T(8,128)S(1)} fusion(bf16[8,1,128,2560]{3,2,1,0:T(8,128)(2,1)} %get-tuple-element.1019, bf16[8,1,128,2560]{3,2,1,0:T(8,128)(2,1)} %get-tuple-element.1020, bf16[128,2,3,16,8]{0,4,3,2,1:T(8,128)(2,1)S(1)} %broadcast_multiply_fusion.8), kind=kOutput, calls=%fused_computation.40.clone.1 | convolution fusion | flops 508559360 | bytes 14614528 | tf_op jit(solution)/shard_map/while/body/eval_jaxpr/mrfig,grmk->gfik/dot_general | solution.py:42
  375.5 3.6 fusion.121
  380.4 6.3 %copy.44 = bf16[128,6,16,40]{3,2,1,0:T(8,128)(2,1)S(1)} copy(bf16[128,6,16,40]{0,2,1,3:T(8,128)(2,1)} %bitcast.165) | data formatting | bytes 1966080 | tf_op jit(solution)/shard_map/reshape | solution.py:186
  386.7 5.8 %reshape.622 = bf16[32,2,7680]{2,1,0:T(2,128)(2,1)} reshape(bf16[128,6,16,40]{3,2,1,0:T(8,128)(2,1)S(1)} %copy.44) | data formatting | bytes 1966080
  392.5 6.4 %all-to-all-start.1 = ((bf16[32,2,7680]{2,1,0:T(2,128)(2,1)}), bf16[32,2,7680]{2,1,0:T(2,128)(2,1)}, u32[]{:S(2)}, u32[]{:S(2)}) async-start(bf16[32,2,7680]{2,1,0:T(2,128)(2,1)} %reshape.622), calls=%async_computation.1 | async-start | bytes 1966080 | tf_op jit(solution)/shard_map/all_to_all | solution.py:187
  399.0 24.1 %all-to-all-done.1 = bf16[32,2,7680]{2,1,0:T(2,128)(2,1)} async-done(((bf16[32,2,7680]{2,1,0:T(2,128)(2,1)}), bf16[32,2,7680]{2,1,0:T(2,128)(2,1)}, u32[]{:S(2)}, u32[]{:S(2)}) %all-to-all-start.1) | async-done | bytes 983072 | tf_op jit(solution)/shard_map/all_to_all | solution.py:187
  423.1 7.1 %reshape.623 = bf16[128,6,16,40]{3,2,1,0:T(8,128)(2,1)S(1)} reshape(bf16[32,2,7680]{2,1,0:T(2,128)(2,1)} %all-to-all-done.1) | data formatting | bytes 1966080
  430.2 3.7 copy.45
  433.9 5.4 all_to_all.30
  441.4 36.0 %while.141 = (s32[]{:T(128)}, bf16[4,6,16,1280]{3,2,1,0:T(8,128)(2,1)S(1)}, s32[4]{0:T(128)S(1)}, bf16[4,640,1280]{2,1,0:T(8,128)(2,1)}, bf16[4,96,640]{2,1,0:T(...) while((s32[]{:T(128)}, ...), condition=%wide.region_11.12_spmd, body=%wide.region_7.11_spmd.sunk | while | flops 63090224 | bytes 5803138 | solution.py:150
  445.3 5.8 %while.143 = (s32[]{:T(128)}, bf16[96,1280]{1,0:T(8,128)(2,1)S(1)}, s32[]{:T(128)}, s32[]{:T(128)}, bf16[640,1280]{1,0:T(8,128)(2,1)S(1)}, /*index=5*/bf16[96,64...) while((s32[]{:T(128)}, bf16[96,1280]{1,0:T(8,128)(2,1)S(1)}, ...), condition=%wide.region_10.10_spmd, body=%wide.region_9.9_spmd.sunk | while | flops 62967300 | bytes 1051303 | solution.py:144
  463.3 2.3 while.143
  471.2 4.6 while.143
  480.0 51.6 %all-gather.2.cloned.1.call-done = bf16[4,6,128,1280]{3,2,1,0:T(8,128)(2,1)} async-done(((bf16[4,6,16,1280]{3,2,1,0:T(8,128)(2,1)}), bf16[4,6,128,1280]{3,2,1,0:T(8,128)(2,1)}) %all-gather.2.cloned.1.call-update) | async-done | bytes 7864336 | tf_op jit(solution)/shard_map/all_gather | solution.py:192
  531.6 7.6 %fusion.74 = bf16[4,6,16,1280]{3,2,1,0:T(8,128)(2,1)} fusion(bf16[4,6,128,1280]{3,2,1,0:T(8,128)(2,1)} %all-gather.2.cloned.1.call-done, f32[4,128,1280]{1,2,0:T(8,128)S(1)} %add_divide_fusion, bf16[128,128]{1,0:T(8,128)(2,1)S(1)} %copy-done, bf16[128,128]{1,0:T(8,128)(2,1)} %param.32, s32[]{:T(128)S(6)} %select_n.229), kind=kOutput, calls=%fused_computation.117 | convolution fusion | flops 1140817920 | bytes 11505668 | tf_op jit(solution)/shard_map/lk,mcki->mcli/dot_general | solution.py:198
  (322 shorter events, 87.3 us)
Async XLA Ops:
  6.5 525.1 %copy-start = (bf16[128,128]{1,0:T(8,128)(2,1)S(1)}, bf16[128,128]{1,0:T(8,128)(2,1)}, u32[]{:S(2)}) copy-start(bf16[128,128]{1,0:T(8,128)(2,1)} %param.31) | copy-start | bytes 98308
  11.2 6.7 %copy-start.4 = (s32[4]{0:T(128)S(1)}, s32[4]{0:T(128)}, u32[]{:S(2)}) copy-start(s32[4]{0:T(128)} %get-tuple-element.1164) | copy-start | bytes 52 | tf_op jit(solution)/shard_map/while
  23.3 1.8 copy-start.4
  30.5 3.0 copy-start.4
  39.0 5.5 %copy-start.4 = (s32[4]{0:T(128)S(1)}, s32[4]{0:T(128)}, u32[]{:S(2)}) copy-start(s32[4]{0:T(128)} %get-tuple-element.1164) | copy-start | bytes 52 | tf_op jit(solution)/shard_map/while
  45.9 18.7 %copy-start.8 = (s32[4]{0:T(128)}, s32[4]{0:T(128)S(1)}, u32[]{:S(2)}) copy-start(s32[4]{0:T(128)S(1)} %get-tuple-element.1251) | copy-start | bytes 52
  64.6 36.8 %all-to-all-start = ((bf16[32,2,7680]{2,1,0:T(2,128)(2,1)}), bf16[32,2,7680]{2,1,0:T(2,128)(2,1)S(1)}, u32[]{:S(2)}, u32[]{:S(2)}) async-start(bf16[32,2,7680]{2,1,0:T(2,128)(2,1)} %reshape.620), calls=%async_computation | async-start | bytes 1966080 | tf_op jit(solution)/shard_map/all_to_all | solution.py:171
  116.5 7.4 %copy-start.3 = (s32[128]{0:T(128)S(1)}, s32[128]{0:T(128)}, u32[]{:S(2)}) copy-start(s32[128]{0:T(128)} %param.26) | copy-start | bytes 1540
  164.2 7.1 %slice-start = ((s8[5242880]{0:T(1024)(128)(4,1)}), s8[4194304]{0:T(1024)(128)(4,1)S(1)}, s32[]{:S(2)}) async-start(s8[5242880]{0:T(1024)(128)(4,1)} %bitcast.151), calls=%async_computation.3 | async-start | bytes 8388608 | tf_op jit(solution)/shard_map/while
  164.2 7.1 %slice-start.2 = ((s8[5242880]{0:T(1024)(128)(4,1)}), s8[4194304]{0:T(1024)(128)(4,1)S(1)}, s32[]{:S(2)}) async-start(s8[5242880]{0:T(1024)(128)(4,1)} %bitcast.153), calls=%async_computation.5 | async-start | bytes 8388608 | tf_op jit(solution)/shard_map/while
  164.3 7.1 %slice-start.1 = ((s8[5242880]{0:T(1024)(128)(4,1)}), s8[1048576]{0:T(1024)(128)(4,1)S(1)}, s32[]{:S(2)}) async-start(s8[5242880]{0:T(1024)(128)(4,1)} %bitcast.151), calls=%async_computation.4 | async-start | bytes 2097152 | tf_op jit(solution)/shard_map/while
  164.3 7.1 %slice-start.3 = ((s8[5242880]{0:T(1024)(128)(4,1)}), s8[1048576]{0:T(1024)(128)(4,1)S(1)}, s32[]{:S(2)}) async-start(s8[5242880]{0:T(1024)(128)(4,1)} %bitcast.153), calls=%async_computation.6 | async-start | bytes 2097152 | tf_op jit(solution)/shard_map/while
  215.2 7.1 %slice-start = ((s8[5242880]{0:T(1024)(128)(4,1)}), s8[4194304]{0:T(1024)(128)(4,1)S(1)}, s32[]{:S(2)}) async-start(s8[5242880]{0:T(1024)(128)(4,1)} %bitcast.151), calls=%async_computation.3 | async-start | bytes 8388608 | tf_op jit(solution)/shard_map/while
  215.2 7.1 %slice-start.2 = ((s8[5242880]{0:T(1024)(128)(4,1)}), s8[4194304]{0:T(1024)(128)(4,1)S(1)}, s32[]{:S(2)}) async-start(s8[5242880]{0:T(1024)(128)(4,1)} %bitcast.153), calls=%async_computation.5 | async-start | bytes 8388608 | tf_op jit(solution)/shard_map/while
  215.3 7.1 %slice-start.1 = ((s8[5242880]{0:T(1024)(128)(4,1)}), s8[1048576]{0:T(1024)(128)(4,1)S(1)}, s32[]{:S(2)}) async-start(s8[5242880]{0:T(1024)(128)(4,1)} %bitcast.151), calls=%async_computation.4 | async-start | bytes 2097152 | tf_op jit(solution)/shard_map/while
  215.3 7.1 %slice-start.3 = ((s8[5242880]{0:T(1024)(128)(4,1)}), s8[1048576]{0:T(1024)(128)(4,1)S(1)}, s32[]{:S(2)}) async-start(s8[5242880]{0:T(1024)(128)(4,1)} %bitcast.153), calls=%async_computation.6 | async-start | bytes 2097152 | tf_op jit(solution)/shard_map/while
  266.3 7.1 %slice-start = ((s8[5242880]{0:T(1024)(128)(4,1)}), s8[4194304]{0:T(1024)(128)(4,1)S(1)}, s32[]{:S(2)}) async-start(s8[5242880]{0:T(1024)(128)(4,1)} %bitcast.151), calls=%async_computation.3 | async-start | bytes 8388608 | tf_op jit(solution)/shard_map/while
  266.3 7.1 %slice-start.2 = ((s8[5242880]{0:T(1024)(128)(4,1)}), s8[4194304]{0:T(1024)(128)(4,1)S(1)}, s32[]{:S(2)}) async-start(s8[5242880]{0:T(1024)(128)(4,1)} %bitcast.153), calls=%async_computation.5 | async-start | bytes 8388608 | tf_op jit(solution)/shard_map/while
  266.3 7.1 %slice-start.1 = ((s8[5242880]{0:T(1024)(128)(4,1)}), s8[1048576]{0:T(1024)(128)(4,1)S(1)}, s32[]{:S(2)}) async-start(s8[5242880]{0:T(1024)(128)(4,1)} %bitcast.151), calls=%async_computation.4 | async-start | bytes 2097152 | tf_op jit(solution)/shard_map/while
  266.3 7.1 %slice-start.3 = ((s8[5242880]{0:T(1024)(128)(4,1)}), s8[1048576]{0:T(1024)(128)(4,1)S(1)}, s32[]{:S(2)}) async-start(s8[5242880]{0:T(1024)(128)(4,1)} %bitcast.153), calls=%async_computation.6 | async-start | bytes 2097152 | tf_op jit(solution)/shard_map/while
  317.3 7.1 %slice-start = ((s8[5242880]{0:T(1024)(128)(4,1)}), s8[4194304]{0:T(1024)(128)(4,1)S(1)}, s32[]{:S(2)}) async-start(s8[5242880]{0:T(1024)(128)(4,1)} %bitcast.151), calls=%async_computation.3 | async-start | bytes 8388608 | tf_op jit(solution)/shard_map/while
  317.3 7.1 %slice-start.2 = ((s8[5242880]{0:T(1024)(128)(4,1)}), s8[4194304]{0:T(1024)(128)(4,1)S(1)}, s32[]{:S(2)}) async-start(s8[5242880]{0:T(1024)(128)(4,1)} %bitcast.153), calls=%async_computation.5 | async-start | bytes 8388608 | tf_op jit(solution)/shard_map/while
  317.3 7.1 %slice-start.1 = ((s8[5242880]{0:T(1024)(128)(4,1)}), s8[1048576]{0:T(1024)(128)(4,1)S(1)}, s32[]{:S(2)}) async-start(s8[5242880]{0:T(1024)(128)(4,1)} %bitcast.151), calls=%async_computation.4 | async-start | bytes 2097152 | tf_op jit(solution)/shard_map/while
  317.4 7.1 %slice-start.3 = ((s8[5242880]{0:T(1024)(128)(4,1)}), s8[1048576]{0:T(1024)(128)(4,1)S(1)}, s32[]{:S(2)}) async-start(s8[5242880]{0:T(1024)(128)(4,1)} %bitcast.153), calls=%async_computation.6 | async-start | bytes 2097152 | tf_op jit(solution)/shard_map/while
  368.3 7.1 %slice-start = ((s8[5242880]{0:T(1024)(128)(4,1)}), s8[4194304]{0:T(1024)(128)(4,1)S(1)}, s32[]{:S(2)}) async-start(s8[5242880]{0:T(1024)(128)(4,1)} %bitcast.151), calls=%async_computation.3 | async-start | bytes 8388608 | tf_op jit(solution)/shard_map/while
  368.3 7.1 %slice-start.2 = ((s8[5242880]{0:T(1024)(128)(4,1)}), s8[4194304]{0:T(1024)(128)(4,1)S(1)}, s32[]{:S(2)}) async-start(s8[5242880]{0:T(1024)(128)(4,1)} %bitcast.153), calls=%async_computation.5 | async-start | bytes 8388608 | tf_op jit(solution)/shard_map/while
  368.4 7.1 %slice-start.1 = ((s8[5242880]{0:T(1024)(128)(4,1)}), s8[1048576]{0:T(1024)(128)(4,1)S(1)}, s32[]{:S(2)}) async-start(s8[5242880]{0:T(1024)(128)(4,1)} %bitcast.151), calls=%async_computation.4 | async-start | bytes 2097152 | tf_op jit(solution)/shard_map/while
  368.4 7.1 %slice-start.3 = ((s8[5242880]{0:T(1024)(128)(4,1)}), s8[1048576]{0:T(1024)(128)(4,1)S(1)}, s32[]{:S(2)}) async-start(s8[5242880]{0:T(1024)(128)(4,1)} %bitcast.153), calls=%async_computation.6 | async-start | bytes 2097152 | tf_op jit(solution)/shard_map/while
  379.4 0.9 copy-start.2
  392.5 30.5 %all-to-all-start.1 = ((bf16[32,2,7680]{2,1,0:T(2,128)(2,1)}), bf16[32,2,7680]{2,1,0:T(2,128)(2,1)}, u32[]{:S(2)}, u32[]{:S(2)}) async-start(bf16[32,2,7680]{2,1,0:T(2,128)(2,1)} %reshape.622), calls=%async_computation.1 | async-start | bytes 1966080 | tf_op jit(solution)/shard_map/all_to_all | solution.py:187
  398.9 132.7 %all-gather.2.cloned.1.call-start = ((), (), s32[]{:S(2)}) async-start(), calls=%async_computation.2 | async-start | bytes 8847360 | tf_op jit(solution)/shard_map/all_gather | solution.py:192
  430.2 9.8 %copy-start.6 = (f32[640]{0:T(1024)S(1)}, f32[640]{0:T(1024)}, u32[]{:S(2)}) copy-start(f32[640]{0:T(1024)} %param.30) | copy-start | bytes 7684
  433.9 7.5 %copy-start.5 = (s32[4]{0:T(128)S(1)}, s32[4]{0:T(128)}, u32[]{:S(2)}) copy-start(s32[4]{0:T(128)} %get-tuple-element.1250) | copy-start | bytes 52
  433.9 7.5 %copy-start.9 = (s32[4]{0:T(128)S(1)}, s32[4]{0:T(128)}, u32[]{:S(2)}) copy-start(s32[4]{0:T(128)} %copy-done.8) | copy-start | bytes 52
  441.4 37.2 %copy-start.7 = (f32[128]{0:T(128)S(1)}, f32[128]{0:T(128)}, u32[]{:S(2)}) copy-start(f32[128]{0:T(128)} %param.33) | copy-start | bytes 1540
  477.4 0.9 copy-start.1
Sparse Core Ops, SparseCore 0:
  478.5 53.0 all-gather.1
where the time goes:
time: 553 us; the launch traced here: 546 us
  local copies, waits for them, and re-layouts  188 us (34%)
  other arithmetic  152 us (27%)
  waiting for transfers between devices  99.8 us (18%)
  matrix products  66 us (12%)
  starting transfers between devices  18.3 us (3%)
  between operations  13.6 us (2%)
  loops' own time  8.43 us (2%)
    another operation x17, other arithmetic  61.9 us
    all_gather x1, waiting for transfers between devices, on_device(): lax.all_gather(projected, 'lev', axis=2, tiled=True)  51.6 us
    sub x5, local copies, waits for them, and re-layouts, trig_rows(): cos_high * cos_low - sin_high * sin_low  40 us
    neg x5, local copies, waits for them, and re-layouts, trig_rows(): sine_part = jnp.where(live_mask, -sine, 0.0)  39.9 us
    sub x5, other arithmetic, trig_rows(): cos_high * cos_low - sin_high * sin_low  34.8 us
    unnamed x22, local copies, waits for them, and re-layouts  32.9 us
    dot_general x5, matrix products, cycle_trip(): jnp.einsum('mrfig,grmk->gfik', weighted, polys, preferred_element_type=jn...  29.1 us
    all_to_all x1, waiting for transfers between devices, on_device(): lax.all_to_all(analysed, 'wave', split_axis=0, concat_axis=3, tiled=True)  24.1 us
  transfers between devices with their start and end apart: 3, of which 3 were waited for; matrix products, arithmetic and copies ran while one was open for 0% of the time, Pallas kernels for 0%

commit v1 on v0

v1 whole, which is shorter than its diff:
```python
import jax
import jax.numpy as jnp
import numpy as np
from jax import lax
from jax.experimental import pallas as pl
from jax.experimental.pallas import tpu as pltpu
from jax.sharding import PartitionSpec as P

MESH = pl.DeviceIdType.MESH
NT = 1280
BF = jnp.bfloat16
F32 = jnp.float32
WAVES = 32
LEVS = 8
DEVS = 256
CYC = 5
SECTIONS = ((0, 0, 0, 96), (0, 1, 96, 128), (1, 1, 0, 64), (1, 2, 64, 128), (2, 2, 0, 32), (2, 3, 32, 128))


def nt_dot(a, b):
    return lax.dot_general(a, b, (((1,), (1,)), ((), ())), preferred_element_type=F32)


def nn_dot(a, b):
    return lax.dot_general(a, b, (((1,), (0,)), ((), ())), preferred_element_type=F32)


def constant_arrays():
    block, row = np.divmod(np.arange(256), 16)
    tile, cyc = np.divmod(np.arange(240), 80)
    pack = (row[:, None] < 15) & (row[:, None] // 5 == tile[None]) & (5 * block[:, None] + row[:, None] % 5 == cyc[None])
    src_u, rest = np.divmod(np.arange(480), 96)
    src_t, src_w = np.divmod(rest, 32)
    in_w, in_row = np.divmod(np.arange(512), 16)
    unpack = (src_w[:, None] == in_w[None]) & (src_t[:, None] * 5 + src_u[:, None] == in_row[None])
    spread = np.arange(96)[:, None] == np.arange(384)[None] % 96
    fu, dest = np.divmod(np.arange(240), 16)
    back = (block[:, None] == dest[None]) & (row[:, None] == fu[None])
    return [x.astype(np.float32) for x in (pack, unpack, spread, back, pack.T, np.eye(256))]


def position():
    return lax.axis_index("wave"), lax.axis_index("lev")


def mirrored(dest):
    return jnp.where(dest < 128, dest, 383 - dest)


def inverse_rows(spec_ref, len_of, rhs):
    column = lax.broadcasted_iota(jnp.int32, (1, NT), 1)
    for idx, (t, m, lo, hi) in enumerate(SECTIONS):
        live = column < len_of(m)
        north = jnp.where(live, 1.0, 0.0).astype(BF)
        south = jnp.where(live, jnp.where(column % 2 == 0, 1.0, -1.0), 0.0).astype(BF)
        for half, factor in ((0, north), (128, south)):
            if lo > 0:
                rhs[idx, half : half + lo, :] = jnp.zeros((lo, NT), BF)
            if hi < 128:
                rhs[idx, half + hi : half + 128, :] = jnp.zeros((128 - hi, NT), BF)
            rhs[idx, half + lo : half + hi, :] = spec_ref[t * 128 + lo : t * 128 + hi, :] * factor


def inverse_dots(leg, rhs, waves_out):
    step = 320
    for t in range(3):
        ma, mb = SECTIONS[2 * t][1], SECTIONS[2 * t + 1][1]

        def block(jc, _):
            rows = pl.ds(pl.multiple_of(jc * step, 64), step)
            out = nt_dot(leg[ma, rows, :], rhs[2 * t]) + nt_dot(leg[mb, rows, :], rhs[2 * t + 1])
            waves_out[t, rows, :] = out.astype(BF)
            return 0

        lax.fori_loop(0, 640 // step, block, 0)


def inverse_pack(pack, waves_out, send):
    def block(g, _):
        rows = pl.ds(pl.multiple_of(g * 80, 16), 80)
        x = jnp.concatenate([waves_out[t, rows, :] for t in range(3)], axis=0)
        y = nn_dot(pack[...], x).astype(BF)
        send[pl.ds(g * 16, 16)] = y[:, :128].reshape(16, 16, 128)
        send[pl.ds(128 + g * 16, 16)] = y[:, 128:].reshape(16, 16, 128)
        return 0

    lax.fori_loop(0, 8, block, 0)


def cos_sin(steps, count):
    turns = jnp.round(steps * (4.0 / count))
    rest = steps - turns * (count * 0.25)
    x = rest * (2.0 * np.pi / count)
    x2 = x * x
    sine = x * (1.0 + x2 * (-1.0 / 6 + x2 * (1.0 / 120 + x2 * (-1.0 / 5040 + x2 * (1.0 / 362880)))))
    cosine = 1.0 + x2 * (-0.5 + x2 * (1.0 / 24 + x2 * (-1.0 / 720 + x2 * (1.0 / 40320))))
    quadrant = turns.astype(jnp.int32) & 3
    swap = (quadrant & 1) == 1
    c = jnp.where(swap, sine, cosine)
    s = jnp.where(swap, cosine, sine)
    c = jnp.where((quadrant == 1) | (quadrant == 2), -c, c)
    s = jnp.where(quadrant >= 2, -s, s)
    return c, s


def cycle_table(wave_col, points, table, low):
    count = jnp.full((1, 128), points, jnp.int32).astype(F32)
    lane = lax.broadcasted_iota(jnp.int32, (1, 128), 1)
    lane_f = lane.astype(F32)
    waves = wave_col[...]
    for half in range(2):
        c, s = cos_sin(waves * (lane_f + 128.0 * half), count)
        low[0, :, half * 128 : half * 128 + 128] = c
        low[1, :, half * 128 : half * 128 + 128] = s
    c_high, s_high = cos_sin(waves * (lane_f * 256.0), count)
    live = 2.0 * waves < count
    c_high = jnp.where(live, c_high, 0.0)
    s_high = jnp.where(live, s_high, 0.0)
    wide = lax.broadcasted_iota(jnp.int32, (1, 256), 1)
    for a in range(10):
        ca = c_high[:, a : a + 1]
        sa = s_high[:, a : a + 1]
        keep = jnp.where(wide + 256 * a < points, 1.0, 0.0)
        cl = low[0] * keep
        sl = low[1] * keep
        cols = slice(a * 256, a * 256 + 256)
        table[0:128, cols] = (cl * ca - sl * sa).astype(BF)
        table[128:256, cols] = (-(sl * ca + cl * sa)).astype(BF)


def gather_waves(recv, unpack, spread, wave_row, fields):
    lane = lax.broadcasted_iota(jnp.int32, (1, 384), 1)
    sections = [jnp.where((lane >= 96 * m) & (lane < 96 * m + 96), 1.0, 0.0).astype(BF) for m in range(4)]
    factor = jnp.where(wave_row[0:1, :] == 0.0, 1.0, 2.0)

    def pair(sp, _):
        first = recv[pl.ds(sp * 64, 32)].reshape(512, 128)
        second = recv[pl.ds(sp * 64 + 32, 32)].reshape(512, 128)
        z = nn_dot(unpack[...], jnp.concatenate([first, second], axis=1)).astype(BF)
        for u in range(CYC):
            pieces = []
            for h in range(2):
                zu = jnp.concatenate(
                    [z[u * 96 + t * 32 : u * 96 + t * 32 + 32, h * 128 : h * 128 + 128] for t in range(3)], axis=1
                )
                pieces += [zu * sections[m] for m in range(4)]
            y = nt_dot(spread[...], jnp.concatenate(pieces, axis=0))
            for h in range(2):
                part = (y[:, h * 128 : h * 128 + 128] * factor).astype(BF)
                for r in range(2):
                    for f in range(3):
                        rows = pl.ds(pl.multiple_of(f * 128 + sp * 32 + h * 16, 16), 16)
                        fields[u, rows, r * 128 : r * 128 + 128] = part[r * 48 + f * 16 : r * 48 + f * 16 + 16, :]
        return 0

    lax.fori_loop(0, 4, pair, 0)


def grid_cycle(u, points, coef_row, table, fields, tend, analysed):
    for a in range(10):
        cols = slice(a * 256, a * 256 + 256)
        g = nn_dot(fields[u], table[:, cols])
        coef = coef_row[:, cols]
        for f in range(3):
            nxt = (f + 1) % 3
            tend[f * 128 : f * 128 + 128, cols] = (
                g[f * 128 : f * 128 + 128] * (coef + g[nxt * 128 : nxt * 128 + 128])
            ).astype(BF)
    total = nt_dot(table[...], tend[...])
    count = jnp.full((1, 384), points, jnp.int32).astype(F32)
    analysed[u] = (total / count).astype(BF)


def pack_return(back, analysed, send):
    def pair(g, _):
        halves = []
        for h in range(2):
            rows = pl.ds(pl.multiple_of(g * 32 + h * 16, 16), 16)
            halves.append(
                jnp.concatenate(
                    [analysed[u, rows, f * 128 : f * 128 + 128] for f in range(3) for u in range(CYC)], axis=0
                )
            )
        y = nn_dot(back[...], jnp.concatenate(halves, axis=1)).astype(BF)
        send[pl.ds(g * 32, 16)] = y[:, :128].reshape(16, 16, 128)
        send[pl.ds(g * 32 + 16, 16)] = y[:, 128:].reshape(16, 16, 128)
        return 0

    lax.fori_loop(0, 8, pair, 0)


def parity_parts(recv, packt, weight_col, parts):
    def block(g, _):
        rows = pl.ds(pl.multiple_of(g * 80, 16), 80)
        x = jnp.concatenate(
            [recv[pl.ds(g * 16, 16)].reshape(256, 128), recv[pl.ds(128 + g * 16, 16)].reshape(256, 128)], axis=1
        )
        z = nn_dot(packt[...], x)
        weight = weight_col[rows, :]
        for f in range(3):
            north = z[f * 80 : f * 80 + 80, :128]
            south = z[f * 80 : f * 80 + 80, 128:]
            parts[f, rows, 0:128] = (weight * (north + south)).astype(BF)
            parts[f, rows, 128:256] = (weight * (north - south)).astype(BF)
        return 0

    lax.fori_loop(0, 8, block, 0)


def forward_modes(leg_m, length, wave, eye, parts, flipped, modes_in, modes_out, depth_col, update):
    for f in range(3):
        t = nt_dot(eye[...], parts[f]).astype(BF)
        flipped[0, f * 128 : f * 128 + 128, :] = t[:128]
        flipped[1, f * 128 : f * 128 + 128, :] = t[128:]
    lane = lax.broadcasted_iota(jnp.int32, (1, 256), 1)
    even_lane = lane % 2 == 0

    def block(ic, _):
        cols = pl.ds(pl.multiple_of(ic * 256, 256), 256)
        polys = leg_m(cols)
        even = nn_dot(flipped[0], polys)
        odd = nn_dot(flipped[1], polys)
        where = lane + ic * 256
        proj = jnp.where(where < length, jnp.where(even_lane, even, odd), 0.0).astype(BF)
        degree = (where + wave).astype(F32)
        depth = depth_col[:, 0:1]
        damp = 1.0 / (1.0 + depth * degree * (degree + 1.0) / float(NT * NT))
        for f in range(3):
            vals = nn_dot(modes_in[...], proj[f * 128 : f * 128 + 128])
            scaled = (vals * damp).astype(BF)
            update[f, :, cols] = nn_dot(modes_out[...], scaled).astype(BF)
        return 0

    lax.fori_loop(0, NT // 256, block, 0)


def kernel_inverse(lens, spec, leg, pack, send, rhs, waves_out):
    w, _ = position()
    inverse_rows(spec, lambda m: lens[w * 4 + m], rhs)
    inverse_dots(leg, rhs, waves_out)
    inverse_pack(pack, waves_out, send)


def kernel_grid(cyc, recv, coef, wave_col, wave_row, unpack, spread, back, send, table, low, fields, tend, analysed):
    w, s = position()
    dest = w * LEVS + s
    gather_waves(recv, unpack, spread, wave_row, fields)

    def cycle(u, _):
        shift = jnp.where(dest < 128, u, 4 - u)
        points = cyc[dest * CYC + shift]
        cycle_table(wave_col, points, table, low)
        grid_cycle(u, points, coef[pl.ds(s * CYC + shift, 1), :], table, fields, tend, analysed)
        return 0

    lax.fori_loop(0, CYC, cycle, 0)
    pack_return(back, analysed, send)


def kernel_forward(
    lens, waves, recv, leg, packt, eye, weight_col, modes_in, modes_out, depth_col, update, polys, parts, flipped, sem
):
    w, s = position()
    m = s // 2
    fetch = pltpu.make_async_copy(leg.at[m], polys, sem)
    fetch.start()
    parity_parts(recv, packt, weight_col, parts)
    fetch.wait()
    forward_modes(
        lambda cols: polys[:, cols],
        lens[w * 4 + m],
        waves[w * 4 + m],
        eye,
        parts,
        flipped,
        modes_in,
        modes_out,
        depth_col,
        update,
    )


def greet(first, second, everyone):
    w, s = position()

    def lev_peer(i, sem):
        pl.semaphore_signal(sem, inc=1, device_id=(w, lax.rem(s + i, LEVS)), device_id_type=MESH)
        return sem

    def wave_peer(i, sem):
        pl.semaphore_signal(sem, inc=1, device_id=(lax.rem(w + i, WAVES), s), device_id_type=MESH)
        return sem

    lax.fori_loop(1, LEVS, lambda i, c: (lev_peer(i, first), c)[1], 0)
    if not everyone:
        pl.semaphore_wait(first, LEVS - 1)
        return
    lax.fori_loop(1, WAVES, lambda i, c: (wave_peer(i, first), c)[1], 0)
    pl.semaphore_wait(first, LEVS - 1 + WAVES - 1)
    lax.fori_loop(1, WAVES, lambda i, c: (wave_peer(i, second), c)[1], 0)
    pl.semaphore_wait(second, WAVES - 1)


def exchange_all(send, recv, send_sem, recv_sem, own_sem, source_slot, my_slot):
    w, s = position()
    own = pltpu.make_async_copy(send.at[source_slot(w, s)], recv.at[my_slot], own_sem)
    own.start()

    def start(i, _):
        tw = lax.rem(w + lax.rem(i, WAVES), WAVES)
        ts = lax.rem(s + i // WAVES, LEVS)
        pltpu.make_async_remote_copy(
            src_ref=send.at[source_slot(tw, ts)],
            dst_ref=recv.at[my_slot],
            send_sem=send_sem,
            recv_sem=recv_sem,
            device_id=(tw, ts),
            device_id_type=MESH,
        ).start()
        return 0

    lax.fori_loop(1, DEVS, start, 0)
    own.wait()
    rest = pl.ds(0, DEVS - 1)
    pltpu.make_async_copy(send.at[rest], send.at[rest], send_sem).wait()
    pltpu.make_async_copy(recv.at[rest], recv.at[rest], recv_sem).wait()


def kernel_to_cycles(send, recv, second, send_sem, recv_sem, own_sem):
    w, s = position()
    greet(pltpu.get_barrier_semaphore(), second, True)
    exchange_all(send, recv, send_sem, recv_sem, own_sem, lambda tw, ts: mirrored(tw * LEVS + ts), s * WAVES + w)


def kernel_to_waves(send, recv, second, send_sem, recv_sem, own_sem):
    w, s = position()
    greet(pltpu.get_barrier_semaphore(), second, True)
    exchange_all(
        send,
        recv,
        send_sem,
        recv_sem,
        own_sem,
        lambda tw, ts: lax.rem(ts, 2) * 128 + (ts // 2) * 32 + tw,
        mirrored(w * LEVS + s),
    )


def kernel_to_levels(update, out, send_sem, recv_sem, own_sem):
    w, s = position()
    greet(pltpu.get_barrier_semaphore(), None, False)
    m, r = s // 2, lax.rem(s, 2)

    def piece(ts):
        return update.at[:, pl.ds(pl.multiple_of(ts * 16, 16), 16), :]

    place = out.at[m, pl.ds(r * 3, 3)]
    own = pltpu.make_async_copy(piece(s), place, own_sem)
    own.start()
    for i in range(1, LEVS):
        ts = lax.rem(s + i, LEVS)
        pltpu.make_async_remote_copy(
            src_ref=piece(ts),
            dst_ref=place,
            send_sem=send_sem.at[i - 1],
            recv_sem=recv_sem.at[i - 1],
            device_id=(w, ts),
            device_id_type=MESH,
        ).start()
    own.wait()
    for i in range(1, LEVS):
        done = pltpu.make_async_remote_copy(
            src_ref=piece(s),
            dst_ref=place,
            send_sem=send_sem.at[i - 1],
            recv_sem=recv_sem.at[i - 1],
            device_id=(w, lax.rem(s + i, LEVS)),
            device_id_type=MESH,
        )
        done.wait_send()
        done.wait_recv()


VM = pl.BlockSpec(memory_space=pltpu.VMEM)
SM = pl.BlockSpec(memory_space=pltpu.SMEM)
ANY = pl.BlockSpec(memory_space=pl.ANY)
LIMIT = 60 * 1024 * 1024


def call(kernel, ins, outs, out_shape, scratch, name, cid=None):
    extra = {} if cid is None else {"collective_id": cid, "has_side_effects": True}
    return pl.pallas_call(
        kernel,
        out_shape=out_shape,
        in_specs=ins,
        out_specs=outs,
        scratch_shapes=scratch,
        name=name,
        compiler_params=pltpu.CompilerParams(vmem_limit_bytes=LIMIT, **extra),
    )


MESSAGES = jax.ShapeDtypeStruct((DEVS, 16, 128), BF)
SEMS = [pltpu.SemaphoreType.REGULAR] + [pltpu.SemaphoreType.DMA] * 3


def inverse_call(lens, spec, leg, pack):
    return call(
        kernel_inverse,
        [SM, VM, VM, VM],
        VM,
        MESSAGES,
        [pltpu.VMEM((6, 256, NT), BF), pltpu.VMEM((3, 640, 256), BF)],
        "inverse",
    )(lens, spec, leg, pack)


def grid_call(cyc, recv, coef, wave_col, wave_row, unpack, spread, back):
    return call(
        kernel_grid,
        [SM] + [VM] * 7,
        VM,
        MESSAGES,
        [
            pltpu.VMEM((256, 2560), BF),
            pltpu.VMEM((2, 128, 256), F32),
            pltpu.VMEM((CYC, 384, 256), BF),
            pltpu.VMEM((384, 2560), BF),
            pltpu.VMEM((CYC, 256, 384), BF),
        ],
        "grid",
    )(cyc, recv, coef, wave_col, wave_row, unpack, spread, back)


def forward_call(lens, waves, recv, leg, packt, eye, weight_col, modes_in, modes_out, depth_col):
    return call(
        kernel_forward,
        [SM, SM, VM, ANY] + [VM] * 6,
        VM,
        jax.ShapeDtypeStruct((3, 128, NT), BF),
        [
            pltpu.VMEM((640, NT), BF),
            pltpu.VMEM((3, 640, 256), BF),
            pltpu.VMEM((2, 384, 640), BF),
            pltpu.SemaphoreType.DMA,
        ],
        "forward",
    )(lens, waves, recv, leg, packt, eye, weight_col, modes_in, modes_out, depth_col)


def side_arrays(wave_ids, cycle_weights, depths):
    order = wave_ids.reshape(32, 4).T.reshape(128).astype(F32)
    wave_col = jnp.broadcast_to(order[:, None], (128, 128))
    wave_row = jnp.broadcast_to(order[None, :], (8, 128))
    weight_col = jnp.broadcast_to(cycle_weights[:, None], (640, 128))
    depth_col = jnp.broadcast_to(depths[:, None], (128, 128))
    return wave_col, wave_row, weight_col, depth_col


def on_device(
    spectral,
    legendre,
    wave_ids,
    trunc_lengths,
    cycle_points,
    grid_coef,
    cycle_weights,
    modes_in,
    modes_out,
    depths,
):
    pack, unpack, spread, back, packt, eye = [jnp.asarray(x, BF) for x in constant_arrays()]
    wave_col, wave_row, weight_col, depth_col = side_arrays(wave_ids, cycle_weights, depths)
    send = inverse_call(trunc_lengths, spectral.reshape(384, NT), legendre, pack)
    recv = call(kernel_to_cycles, [VM], VM, MESSAGES, SEMS, "to_cycles", 0)(send)
    send = grid_call(cycle_points, recv, grid_coef, wave_col, wave_row, unpack, spread, back)
    recv = call(kernel_to_waves, [VM], VM, MESSAGES, SEMS, "to_waves", 1)(send)
    update = forward_call(
        trunc_lengths, wave_ids, recv, legendre, packt, eye, weight_col, modes_in, modes_out, depth_col
    )
    return call(
        kernel_to_levels,
        [VM],
        ANY,
        jax.ShapeDtypeStruct((4, 6, 16, NT), BF),
        [pltpu.SemaphoreType.DMA((LEVS - 1,)), pltpu.SemaphoreType.DMA((LEVS - 1,)), pltpu.SemaphoreType.DMA],
        "to_levels",
        2,
    )(update)


def solution(mesh):
    placed = (
        P("wave", None, "lev", None),
        P("wave", None, None),
        P(),
        P(),
        P(),
        P("wave", None),
        P(),
        P(),
        P(),
        P(),
    )
    return jax.shard_map(
        on_device,
        mesh=mesh,
        in_specs=placed,
        out_specs=P("wave", None, "lev", None),
        check_vma=False,
    )
```

time: 553 us -> 138 us (0.25); the launches traced: 546 us -> 137 us
  local copies, waits for them, and re-layouts: 188 us -> 5.37 us
  other arithmetic: 152 us -> 0.66 us
  Pallas kernels: 0 us -> 131 us
  waiting for transfers between devices: 99.8 us -> 0 us
  matrix products: 66 us -> 0 us
  starting transfers between devices: 18.3 us -> 0 us
  between operations: 13.6 us -> 0.05 us
  loops' own time: 8.43 us -> 0 us
    pallas_call x0 -> x6, Pallas kernels: none -> 131 us  [the longest x1 44.3 us: on_device(): call(kernel_to_cycles, [VM], VM, MESSAGES, SEMS, 'to_cycles', 0)(send)]
    dot_general x59 -> x0, matrix products: 66 us -> none  [the longest x5 29.1 us: cycle_trip(): jnp.einsum('mrfig,grmk->gfik', weighted, polys, preferred_element_type=jn...]
    another operation x17 -> x0, other arithmetic: 61.9 us -> none
    all_gather x1 -> x0, waiting for transfers between devices: 51.6 us -> none  [on_device(): lax.all_gather(projected, 'lev', axis=2, tiled=True)]
    all_to_all x2 -> x0, waiting for transfers between devices: 48.2 us -> none  [the longest x1 24.1 us: on_device(): lax.all_to_all(analysed, 'wave', split_axis=0, concat_axis=3, tiled=True)]
    sub x5 -> x0, local copies, waits for them, and re-layouts: 40 us -> none  [trig_rows(): cos_high * cos_low - sin_high * sin_low]
    neg x5 -> x0, local copies, waits for them, and re-layouts: 39.9 us -> none  [trig_rows(): sine_part = jnp.where(live_mask, -sine, 0.0)]
    sub x9 -> x0, other arithmetic: 34.9 us -> none  [the longest x5 34.8 us: trig_rows(): cos_high * cos_low - sin_high * sin_low]
  transfers between devices with their start and end apart: 3 -> 0, of which waited for: 3 -> 0; matrix products, arithmetic and copies ran while one was open for 0% -> 0% of each run, Pallas kernels for 0% -> 0%
where the time goes in v1:
time: 138 us; the launch traced here: 137 us
  Pallas kernels  131 us (95%)
  local copies, waits for them, and re-layouts  5.37 us (4%)
    pallas_call x1, Pallas kernels, on_device(): call(kernel_to_cycles, [VM], VM, MESSAGES, SEMS, 'to_cycles', 0)(send)  44.3 us
    pallas_call x1, Pallas kernels, on_device(): recv = call(kernel_to_waves, [VM], VM, MESSAGES, SEMS, 'to_waves', 1)(send)  35.4 us
    pallas_call x1, Pallas kernels, grid_call(): call(kernel_grid, [SM] + [VM] * 7, VM, MESSAGES, [pltpu.VMEM((256, 2560),...  17.3 us
    pallas_call x1, Pallas kernels, on_device(): call(kernel_to_levels, [VM], ANY, jax.ShapeDtypeStruct((4, 6, 16, NT), BF...  16.3 us
    pallas_call x1, Pallas kernels, inverse_call(): call(kernel_inverse, [SM, VM, VM, VM], VM, MESSAGES, [pltpu.VMEM((6, 256,...  9.68 us
    pallas_call x1, Pallas kernels, forward_call(): call(kernel_forward, [SM, SM, VM, ANY] + [VM] * 6, VM, jax.ShapeDtypeStru...  8.34 us

profile of v1, /device:TPU:1, one launch (start us, length us, event | category | flops | bytes accessed | tf_op | source)
XLA Modules:
  0.0 137.4 jit_solution(7712817595512844051)
XLA Ops:
  0.0 0.7 convert_element_type.20
  0.7 0.1 convert_element_type.21
  0.8 0.1 copy.18
  0.8 0.1 convert_element_type.23
  0.9 0.7 broadcast_in_dim.8.wave_col
  1.7 0.6 broadcast_in_dim.9.wave_row
  2.2 0.0 copy-start
  2.3 0.0 copy-start.1
  2.3 9.7 %inverse.1.send = bf16[256,16,128]{2,1,0:T(8,128)(2,1)} custom-call(s32[128]{0:T(128)} %lens.3, bf16[384,1280]{1,0:T(8,128)(2,1)} %bitcast.2, bf16[4,640,1280]{2,1,0:T(8,128)(2,1)} %leg.3, bf16[256,240]{1,0:T(8,128)(2,1)} %constant.12.clone.pack), custom_call_target="tpu_custom_call" | custom-call | tf_op jit(solution)/shard_map/inverse/pallas_call | solution.py:408
  11.9 44.3 %to_cycles.1.recv = bf16[256,16,128]{2,1,0:T(8,128)(2,1)} custom-call(bf16[256,16,128]{2,1,0:T(8,128)(2,1)} %inverse.1.send), custom_call_target="tpu_custom_call" | custom-call | tf_op jit(solution)/shard_map/to_cycles/pallas_call | solution.py:475
  56.2 17.3 %grid.1.send = bf16[256,16,128]{2,1,0:T(8,128)(2,1)} custom-call(s32[1280]{0:T(1024)} %cyc.1, bf16[256,16,128]{2,1,0:T(8,128)(2,1)} %to_cycles.1.recv, f32[40,2560]{1,0:T(8,128)} %coef.1, f32[128,128]{1,0:T(8,128)} %broadcast_in_dim.8.wave_col, f32[8,128]{1,0:T(8,128)} %broadcast_in_dim.9.wave_row, bf16[480,512]{1,0:T(8,128)(2,1)} %constant.13.clone.unpack, ...), custom_call_target="tpu_custom_call" | custom-call | tf_op jit(solution)/shard_map/grid/pallas_call | solution.py:419
  73.6 35.4 %to_waves.1.recv = bf16[256,16,128]{2,1,0:T(8,128)(2,1)} custom-call(bf16[256,16,128]{2,1,0:T(8,128)(2,1)} %grid.1.send), custom_call_target="tpu_custom_call" | custom-call | tf_op jit(solution)/shard_map/to_waves/pallas_call | solution.py:477
  108.9 0.0 copy-done
  109.0 0.9 broadcast_in_dim.10.weight_col
  109.8 0.0 copy-done.1
  109.8 0.7 broadcast_in_dim.11.depth_col
  110.5 8.3 %forward.1.update = bf16[3,128,1280]{2,1,0:T(8,128)(2,1)} custom-call(s32[128]{0:T(128)} %lens.3, s32[128]{0:T(128)} %waves.1, bf16[256,16,128]{2,1,0:T(8,128)(2,1)} %to_waves.1.recv, bf16[4,640,1280]{2,1,0:T(8,128)(2,1)} %leg.3, bf16[240,256]{1,0:T(8,128)(2,1)} %constant.16.clone.packt, bf16[256,256]{1,0:T(8,128)(2,1)} %constant.17.clone.eye, ...), custom_call_target="tpu_custom_call" | custom-call | tf_op jit(solution)/shard_map/forward/pallas_call | solution.py:436
  118.9 16.3 %to_levels.1 = bf16[4,6,16,1280]{3,2,1,0:T(8,128)(2,1)} custom-call(bf16[3,128,1280]{2,1,0:T(8,128)(2,1)} %forward.1.update), custom_call_target="tpu_custom_call" | custom-call | tf_op jit(solution)/shard_map/to_levels/pallas_call | solution.py:481
  135.2 2.2 %copy.20 = bf16[4,6,16,1280]{3,2,1,0:T(8,128)(2,1)} copy(bf16[4,6,16,1280]{3,2,1,0:T(8,128)(2,1)} %to_levels.1) | data formatting | bytes 1966080
Async XLA Ops:
  2.2 106.7 %copy-start = (f32[640]{0:T(1024)S(1)}, f32[640]{0:T(1024)}, u32[]{:S(2)}) copy-start(f32[640]{0:T(1024)} %param.22) | copy-start | bytes 7684
  2.3 107.6 %copy-start.1 = (f32[128]{0:T(128)S(1)}, f32[128]{0:T(128)}, u32[]{:S(2)}) copy-start(f32[128]{0:T(128)} %param.25) | copy-start | bytes 1540

commit v2 on v1

v2 whole, which is shorter than its diff:
```python
import jax
import jax.numpy as jnp
import numpy as np
from jax import lax
from jax.experimental import pallas as pl
from jax.experimental.pallas import tpu as pltpu
from jax.sharding import PartitionSpec as P

MESH = pl.DeviceIdType.MESH
NT = 1280
BF = jnp.bfloat16
F32 = jnp.float32
WAVES = 32
LEVS = 8
DEVS = 256
CYC = 5
SECTIONS = ((0, 0, 0, 96), (0, 1, 96, 128), (1, 1, 0, 64), (1, 2, 64, 128), (2, 2, 0, 32), (2, 3, 32, 128))


def nt_dot(a, b):
    return lax.dot_general(a, b, (((1,), (1,)), ((), ())), preferred_element_type=F32)


def nn_dot(a, b):
    return lax.dot_general(a, b, (((1,), (0,)), ((), ())), preferred_element_type=F32)


def constant_arrays():
    block, row = np.divmod(np.arange(256), 16)
    tile, cyc = np.divmod(np.arange(240), 80)
    pack = (row[:, None] < 15) & (row[:, None] // 5 == tile[None]) & (5 * block[:, None] + row[:, None] % 5 == cyc[None])
    src_u, rest = np.divmod(np.arange(480), 96)
    src_t, src_w = np.divmod(rest, 32)
    in_w, in_row = np.divmod(np.arange(512), 16)
    unpack = (src_w[:, None] == in_w[None]) & (src_t[:, None] * 5 + src_u[:, None] == in_row[None])
    spread = np.arange(96)[:, None] == np.arange(384)[None] % 96
    fu, dest = np.divmod(np.arange(240), 16)
    back = (block[:, None] == dest[None]) & (row[:, None] == fu[None])
    return [x.astype(np.float32) for x in (pack, unpack, spread, back, pack.T, np.eye(256))]


def position():
    return lax.axis_index("wave"), lax.axis_index("lev")


def shifted(dz, dy, dx, dc):
    w, s = position()
    tw = lax.rem(w // 4 + dz, 8) * 4 + lax.rem(w + dy, 4)
    return tw, lax.rem(s // 2 + dx, 4) * 2 + lax.rem(s + dc, 2)


def mirrored(dest):
    return jnp.where(dest < 128, dest, 383 - dest)


def inverse_rows(spec_ref, len_of, rhs):
    column = lax.broadcasted_iota(jnp.int32, (1, NT), 1)
    for idx, (t, m, lo, hi) in enumerate(SECTIONS):
        live = column < len_of(m)
        north = jnp.where(live, 1.0, 0.0).astype(BF)
        south = jnp.where(live, jnp.where(column % 2 == 0, 1.0, -1.0), 0.0).astype(BF)
        for half, factor in ((0, north), (128, south)):
            if lo > 0:
                rhs[idx, half : half + lo, :] = jnp.zeros((lo, NT), BF)
            if hi < 128:
                rhs[idx, half + hi : half + 128, :] = jnp.zeros((128 - hi, NT), BF)
            rhs[idx, half + lo : half + hi, :] = spec_ref[t * 128 + lo : t * 128 + hi, :] * factor


def inverse_dots(t, leg, rhs, waves_out):
    step = 320
    ma, mb = SECTIONS[2 * t][1], SECTIONS[2 * t + 1][1]

    def block(jc, _):
        rows = pl.ds(pl.multiple_of(jc * step, 64), step)
        out = nt_dot(leg[ma, rows, :], rhs[2 * t]) + nt_dot(leg[mb, rows, :], rhs[2 * t + 1])
        waves_out[t, rows, :] = out.astype(BF)
        return 0

    lax.fori_loop(0, 640 // step, block, 0)


def inverse_pack(pack, waves_out, send):
    def block(g, _):
        rows = pl.ds(pl.multiple_of(g * 80, 16), 80)
        x = jnp.concatenate([waves_out[t, rows, :] for t in range(3)], axis=0)
        y = nn_dot(pack[...], x).astype(BF)
        send[pl.ds(g * 16, 16)] = y[:, :128].reshape(16, 16, 128)
        send[pl.ds(128 + g * 16, 16)] = y[:, 128:].reshape(16, 16, 128)
        return 0

    lax.fori_loop(0, 8, block, 0)


def cos_sin(steps, count):
    turns = jnp.round(steps * (4.0 / count))
    rest = steps - turns * (count * 0.25)
    x = rest * (2.0 * np.pi / count)
    x2 = x * x
    sine = x * (1.0 + x2 * (-1.0 / 6 + x2 * (1.0 / 120 + x2 * (-1.0 / 5040 + x2 * (1.0 / 362880)))))
    cosine = 1.0 + x2 * (-0.5 + x2 * (1.0 / 24 + x2 * (-1.0 / 720 + x2 * (1.0 / 40320))))
    quadrant = turns.astype(jnp.int32) & 3
    swap = (quadrant & 1) == 1
    c = jnp.where(swap, sine, cosine)
    s = jnp.where(swap, cosine, sine)
    c = jnp.where((quadrant == 1) | (quadrant == 2), -c, c)
    s = jnp.where(quadrant >= 2, -s, s)
    return c, s


def cycle_table(u, wave_col, points, table, low):
    count = jnp.full((1, 128), points, jnp.int32).astype(F32)
    lane = lax.broadcasted_iota(jnp.int32, (1, 128), 1)
    lane_f = lane.astype(F32)
    waves = wave_col[...]
    for half in range(2):
        c, s = cos_sin(waves * (lane_f + 128.0 * half), count)
        low[0, :, half * 128 : half * 128 + 128] = c
        low[1, :, half * 128 : half * 128 + 128] = s
    c_high, s_high = cos_sin(waves * (lane_f * 256.0), count)
    live = 2.0 * waves < count
    c_high = jnp.where(live, c_high, 0.0)
    s_high = jnp.where(live, s_high, 0.0)
    wide = lax.broadcasted_iota(jnp.int32, (1, 256), 1)
    for a in range(10):
        ca = c_high[:, a : a + 1]
        sa = s_high[:, a : a + 1]
        keep = jnp.where(wide + 256 * a < points, 1.0, 0.0)
        cl = low[0] * keep
        sl = low[1] * keep
        cols = slice(a * 256, a * 256 + 256)
        table[u, 0:128, cols] = (cl * ca - sl * sa).astype(BF)
        table[u, 128:256, cols] = (-(sl * ca + cl * sa)).astype(BF)


def gather_waves(recv, unpack, spread, wave_row, fields):
    lane = lax.broadcasted_iota(jnp.int32, (1, 384), 1)
    sections = [jnp.where((lane >= 96 * m) & (lane < 96 * m + 96), 1.0, 0.0).astype(BF) for m in range(4)]
    factor = jnp.where(wave_row[0:1, :] == 0.0, 1.0, 2.0)

    def pair(sp, _):
        first = recv[pl.ds(sp * 64, 32)].reshape(512, 128)
        second = recv[pl.ds(sp * 64 + 32, 32)].reshape(512, 128)
        z = nn_dot(unpack[...], jnp.concatenate([first, second], axis=1)).astype(BF)
        for u in range(CYC):
            pieces = []
            for h in range(2):
                zu = jnp.concatenate(
                    [z[u * 96 + t * 32 : u * 96 + t * 32 + 32, h * 128 : h * 128 + 128] for t in range(3)], axis=1
                )
                pieces += [zu * sections[m] for m in range(4)]
            y = nt_dot(spread[...], jnp.concatenate(pieces, axis=0))
            for h in range(2):
                part = (y[:, h * 128 : h * 128 + 128] * factor).astype(BF)
                for r in range(2):
                    for f in range(3):
                        rows = pl.ds(pl.multiple_of(f * 128 + sp * 32 + h * 16, 16), 16)
                        fields[u, rows, r * 128 : r * 128 + 128] = part[r * 48 + f * 16 : r * 48 + f * 16 + 16, :]
        return 0

    lax.fori_loop(0, 4, pair, 0)


def grid_cycle(u, points, coef_row, table, fields, tend, analysed):
    for a in range(10):
        cols = slice(a * 256, a * 256 + 256)
        g = nn_dot(fields[u], table[u, :, cols])
        coef = coef_row[:, cols]
        for f in range(3):
            nxt = (f + 1) % 3
            tend[f * 128 : f * 128 + 128, cols] = (
                g[f * 128 : f * 128 + 128] * (coef + g[nxt * 128 : nxt * 128 + 128])
            ).astype(BF)
    total = nt_dot(table[u], tend[...])
    count = jnp.full((1, 384), points, jnp.int32).astype(F32)
    analysed[u] = (total / count).astype(BF)


def pack_return(back, analysed, send):
    def pair(g, _):
        halves = []
        for h in range(2):
            rows = pl.ds(pl.multiple_of(g * 32 + h * 16, 16), 16)
            halves.append(
                jnp.concatenate(
                    [analysed[u, rows, f * 128 : f * 128 + 128] for f in range(3) for u in range(CYC)], axis=0
                )
            )
        y = nn_dot(back[...], jnp.concatenate(halves, axis=1)).astype(BF)
        send[pl.ds(g * 32, 16)] = y[:, :128].reshape(16, 16, 128)
        send[pl.ds(g * 32 + 16, 16)] = y[:, 128:].reshape(16, 16, 128)
        return 0

    lax.fori_loop(0, 8, pair, 0)


def parity_parts(recv, packt, weight_col, parts):
    def block(g, _):
        rows = pl.ds(pl.multiple_of(g * 80, 16), 80)
        x = jnp.concatenate(
            [recv[pl.ds(g * 16, 16)].reshape(256, 128), recv[pl.ds(128 + g * 16, 16)].reshape(256, 128)], axis=1
        )
        z = nn_dot(packt[...], x)
        weight = weight_col[rows, :]
        for f in range(3):
            north = z[f * 80 : f * 80 + 80, :128]
            south = z[f * 80 : f * 80 + 80, 128:]
            parts[f, rows, 0:128] = (weight * (north + south)).astype(BF)
            parts[f, rows, 128:256] = (weight * (north - south)).astype(BF)
        return 0

    lax.fori_loop(0, 8, block, 0)


def forward_modes(leg_m, length, wave, eye, parts, flipped, modes_in, modes_out, depth_col, update):
    for f in range(3):
        t = nt_dot(eye[...], parts[f]).astype(BF)
        flipped[0, f * 128 : f * 128 + 128, :] = t[:128]
        flipped[1, f * 128 : f * 128 + 128, :] = t[128:]
    lane = lax.broadcasted_iota(jnp.int32, (1, 256), 1)
    even_lane = lane % 2 == 0

    def block(ic, _):
        cols = pl.ds(pl.multiple_of(ic * 256, 256), 256)
        polys = leg_m(cols)
        even = nn_dot(flipped[0], polys)
        odd = nn_dot(flipped[1], polys)
        where = lane + ic * 256
        proj = jnp.where(where < length, jnp.where(even_lane, even, odd), 0.0).astype(BF)
        degree = (where + wave).astype(F32)
        depth = depth_col[:, 0:1]
        damp = 1.0 / (1.0 + depth * degree * (degree + 1.0) / float(NT * NT))
        for f in range(3):
            vals = nn_dot(modes_in[...], proj[f * 128 : f * 128 + 128])
            scaled = (vals * damp).astype(BF)
            update[f, :, cols] = nn_dot(modes_out[...], scaled).astype(BF)
        return 0

    lax.fori_loop(0, NT // 256, block, 0)


def column_of(row):
    return jnp.transpose(jnp.broadcast_to(row, (128, 128)))


def side_columns(waves_row, weights_row, depths_row, wave_col, wave_row, weight_col, depth_col):
    place = lax.broadcasted_iota(jnp.int32, (128, 128), 0)
    slot = lax.broadcasted_iota(jnp.int32, (128, 128), 1)
    order = jnp.where((place % 32) * 4 + place // 32 == slot, 1.0, 0.0).astype(BF)
    rows = jnp.broadcast_to(waves_row[...], (128, 128))
    high = (rows // 32).astype(F32).astype(BF)
    low = (rows % 32).astype(F32).astype(BF)
    column = nt_dot(order, high) * 32.0 + nt_dot(order, low)
    wave_col[...] = column
    wave_row[...] = jnp.transpose(column)[0:8]
    for i in range(5):
        weight_col[i * 128 : i * 128 + 128, :] = column_of(weights_row[:, i * 128 : i * 128 + 128])
    depth_col[...] = column_of(depths_row[...])


def send_all(send, recv, send_sem, recv_sem, own_sem, source_slot, my_slot):
    w, s = position()
    pltpu.make_async_copy(send.at[source_slot(w, s)], recv.at[my_slot], own_sem).start()

    def start(i, _):
        tw = lax.rem(w + lax.rem(i, WAVES), WAVES)
        ts = lax.rem(s + i // WAVES, LEVS)
        pltpu.make_async_remote_copy(
            src_ref=send.at[source_slot(tw, ts)],
            dst_ref=recv.at[my_slot],
            send_sem=send_sem,
            recv_sem=recv_sem,
            device_id=(tw, ts),
            device_id_type=MESH,
        ).start()
        return 0

    lax.fori_loop(1, DEVS, start, 0)


def wait_all(send, recv, send_sem, recv_sem, own_sem):
    rest = pl.ds(0, DEVS - 1)
    pltpu.make_async_copy(send.at[0], recv.at[0], own_sem).wait()
    pltpu.make_async_copy(send.at[rest], send.at[rest], send_sem).wait()
    pltpu.make_async_copy(recv.at[rest], recv.at[rest], recv_sem).wait()


def signal_peers(sem, peers):
    for peer in peers:
        pl.semaphore_signal(sem, inc=1, device_id=shifted(*peer), device_id_type=MESH)


LEV_PEERS = [(0, 0, dx, dc) for dx in range(4) for dc in range(2) if dx or dc]
Y_PEERS = [(0, dy, 0, 0) for dy in range(1, 4)]
Z_PEERS = [(dz, 0, 0, 0) for dz in range(1, 8)]
N_LATE = 6


def whole(
    lens,
    waves,
    cyc,
    spec_hbm,
    leg_hbm,
    pack_hbm,
    coef_hbm,
    unpack_hbm,
    spread_hbm,
    back_hbm,
    packt_hbm,
    eye_hbm,
    waves_row,
    weights_row,
    depths_row,
    modes_in,
    modes_out,
    out,
    spec,
    leg,
    pack,
    coef,
    unpack,
    spread,
    back,
    packt,
    eye,
    rhs,
    waves_out,
    send_a,
    recv_a,
    table,
    low,
    fields,
    tend,
    analysed,
    send_b,
    recv_b,
    parts,
    flipped,
    update,
    wave_col,
    wave_row,
    weight_col,
    depth_col,
    load_sem,
    late_sem,
    y_sem,
    z_sem,
    sems_a,
    sems_b,
    sems_c,
):
    w, s = position()
    dest = w * LEVS + s
    m, r = s // 2, lax.rem(s, 2)
    barrier = pltpu.get_barrier_semaphore()

    loads = [pltpu.make_async_copy(spec_hbm, spec, load_sem.at[0])]
    loads += [pltpu.make_async_copy(leg_hbm.at[i], leg.at[i], load_sem.at[1 + i]) for i in range(4)]
    loads += [pltpu.make_async_copy(pack_hbm, pack, load_sem.at[5])]
    late = [
        pltpu.make_async_copy(a, b, late_sem.at[i])
        for i, (a, b) in enumerate(
            [
                (coef_hbm, coef),
                (unpack_hbm, unpack),
                (spread_hbm, spread),
                (back_hbm, back),
                (packt_hbm, packt),
                (eye_hbm, eye),
            ]
        )
    ]
    for copy in loads + late:
        copy.start()

    signal_peers(barrier, LEV_PEERS + Y_PEERS + Z_PEERS)
    loads[0].wait()
    inverse_rows(spec, lambda i: lens[w * 4 + i], rhs)
    loads[1].wait()
    loads[2].wait()
    inverse_dots(0, leg, rhs, waves_out)
    pl.semaphore_wait(barrier, len(LEV_PEERS + Y_PEERS + Z_PEERS))
    signal_peers(y_sem, Y_PEERS)
    loads[3].wait()
    inverse_dots(1, leg, rhs, waves_out)
    pl.semaphore_wait(y_sem, len(Y_PEERS))
    signal_peers(z_sem, Z_PEERS)
    loads[4].wait()
    inverse_dots(2, leg, rhs, waves_out)
    loads[5].wait()
    inverse_pack(pack, waves_out, send_a)
    pl.semaphore_wait(z_sem, len(Z_PEERS))

    a_sems = [sems_a.at[i] for i in range(3)]
    send_all(send_a, recv_a, *a_sems, lambda tw, ts: mirrored(tw * LEVS + ts), s * WAVES + w)

    side_columns(waves_row, weights_row, depths_row, wave_col, wave_row, weight_col, depth_col)

    def shift(u):
        return jnp.where(dest < 128, u, 4 - u)

    def make_table(u, _):
        cycle_table(u, wave_col, cyc[dest * CYC + shift(u)], table, low)
        return 0

    lax.fori_loop(0, CYC, make_table, 0)
    for copy in late:
        copy.wait()
    wait_all(send_a, recv_a, *a_sems)

    gather_waves(recv_a, unpack, spread, wave_row, fields)

    def cycle(u, _):
        points = cyc[dest * CYC + shift(u)]
        grid_cycle(u, points, coef[pl.ds(s * CYC + shift(u), 1), :], table, fields, tend, analysed)
        return 0

    lax.fori_loop(0, CYC, cycle, 0)
    pack_return(back, analysed, send_b)
    b_sems = [sems_b.at[i] for i in range(3)]
    send_all(
        send_b, recv_b, *b_sems, lambda tw, ts: lax.rem(ts, 2) * 128 + (ts // 2) * 32 + tw, mirrored(w * LEVS + s)
    )
    wait_all(send_b, recv_b, *b_sems)

    parity_parts(recv_b, packt, weight_col, parts)
    forward_modes(
        lambda cols: leg[m, :, cols],
        lens[w * 4 + m],
        waves[w * 4 + m],
        eye,
        parts,
        flipped,
        modes_in,
        modes_out,
        depth_col,
        update,
    )

    def piece(ts):
        return update.at[:, pl.ds(pl.multiple_of(ts * 16, 16), 16), :]

    place = out.at[m, pl.ds(r * 3, 3)]
    for i in range(1, LEVS):
        ts = lax.rem(s + i, LEVS)
        pltpu.make_async_remote_copy(
            src_ref=piece(ts),
            dst_ref=place,
            send_sem=sems_c.at[0],
            recv_sem=sems_c.at[1],
            device_id=(w, ts),
            device_id_type=MESH,
        ).start()
    pltpu.make_async_copy(piece(s), place, sems_c.at[1]).start()
    sent = update.at[:, 0:112, :]
    pltpu.make_async_copy(sent, sent, sems_c.at[0]).wait()
    pltpu.make_async_copy(out, out, sems_c.at[1]).wait()


VM = pl.BlockSpec(memory_space=pltpu.VMEM)
SM = pl.BlockSpec(memory_space=pltpu.SMEM)
ANY = pl.BlockSpec(memory_space=pl.ANY)


def on_device(
    spectral,
    legendre,
    wave_ids,
    trunc_lengths,
    cycle_points,
    grid_coef,
    cycle_weights,
    modes_in,
    modes_out,
    depths,
):
    pack, unpack, spread, back, packt, eye = [jnp.asarray(x, BF) for x in constant_arrays()]
    vmem = pltpu.VMEM
    return pl.pallas_call(
        whole,
        out_shape=jax.ShapeDtypeStruct((4, 6, 16, NT), BF),
        in_specs=[SM] * 3 + [ANY] * 9 + [VM] * 5,
        out_specs=ANY,
        scratch_shapes=[
            vmem((384, NT), BF),
            vmem((4, 640, NT), BF),
            vmem((256, 240), BF),
            vmem((40, 2560), F32),
            vmem((480, 512), BF),
            vmem((96, 384), BF),
            vmem((256, 240), BF),
            vmem((240, 256), BF),
            vmem((256, 256), BF),
            vmem((6, 256, NT), BF),
            vmem((3, 640, 256), BF),
            vmem((DEVS, 16, 128), BF),
            vmem((DEVS, 16, 128), BF),
            vmem((CYC, 256, 2560), BF),
            vmem((2, 128, 256), F32),
            vmem((CYC, 384, 256), BF),
            vmem((384, 2560), BF),
            vmem((CYC, 256, 384), BF),
            vmem((DEVS, 16, 128), BF),
            vmem((DEVS, 16, 128), BF),
            vmem((3, 640, 256), BF),
            vmem((2, 384, 640), BF),
            vmem((3, 128, NT), BF),
            vmem((128, 128), F32),
            vmem((8, 128), F32),
            vmem((640, 128), F32),
            vmem((128, 128), F32),
            pltpu.SemaphoreType.DMA((6,)),
            pltpu.SemaphoreType.DMA((N_LATE,)),
            pltpu.SemaphoreType.REGULAR,
            pltpu.SemaphoreType.REGULAR,
            pltpu.SemaphoreType.DMA((3,)),
            pltpu.SemaphoreType.DMA((3,)),
            pltpu.SemaphoreType.DMA((2,)),
        ],
        name="whole",
        compiler_params=pltpu.CompilerParams(
            vmem_limit_bytes=56 * 1024 * 1024, collective_id=0, has_side_effects=True
        ),
    )(
        trunc_lengths,
        wave_ids,
        cycle_points,
        spectral.reshape(384, NT),
        legendre,
        pack,
        grid_coef,
        unpack,
        spread,
        back,
        packt,
        eye,
        wave_ids.reshape(1, 128),
        cycle_weights.reshape(1, 640),
        depths.reshape(1, 128),
        modes_in,
        modes_out,
    )


def solution(mesh):
    placed = (
        P("wave", None, "lev", None),
        P("wave", None, None),
        P(),
        P(),
        P(),
        P("wave", None),
        P(),
        P(),
        P(),
        P(),
    )
    return jax.shard_map(
        on_device,
        mesh=mesh,
        in_specs=placed,
        out_specs=P("wave", None, "lev", None),
        check_vma=False,
    )
```

time: 138 us -> 104 us (0.75)
  Pallas kernels: 131 us -> 100 us
  local copies, waits for them, and re-layouts: 5.37 us -> 3.48 us
    pallas_call x6 -> x1, Pallas kernels: 131 us -> 100 us  [on_device(): pl.pallas_call(whole, out_shape=jax.ShapeDtypeStruct((4, 6, 16, NT), BF),...]
    broadcast_in_dim x4 -> x0, local copies, waits for them, and re-layouts: 2.9 us -> none  [the longest x1 0.87 us: side_arrays(): weight_col = jnp.broadcast_to(cycle_weights[:, None], (640, 128))]
where the time goes in v2:
time: 104 us
  Pallas kernels  100 us (96%)
  local copies, waits for them, and re-layouts  3.48 us (3%)
    pallas_call x1, Pallas kernels, on_device(): pl.pallas_call(whole, out_shape=jax.ShapeDtypeStruct((4, 6, 16, NT), BF),...  100 us
    unnamed x1, local copies, waits for them, and re-layouts  2.21 us

profile of v2, /device:TPU:1, one launch (start us, length us, event | category | flops | bytes accessed | tf_op | source)
XLA Modules:
  0.0 103.7 jit_solution(15740074168459429515)
XLA Ops:
  0.0 1.3 %reshape.14.weights_row = f32[1,640]{1,0:T(1,128)} reshape(f32[640]{0:T(1024)} %param.22) | data formatting | bytes 5120 | tf_op jit(solution)/shard_map/reshape | solution.py:539
  1.3 100.2 %whole.1 = bf16[4,6,16,1280]{3,2,1,0:T(8,128)(2,1)} custom-call(s32[128]{0:T(128)} %lens.1, s32[128]{0:T(128)} %waves.1, s32[1280]{0:T(1024)} %cyc.1, bf16[384,1280]{1,0:T(8,128)(2,1)} %bitcast.3, bf16[4,640,1280]{2,1,0:T(8,128)(2,1)} %leg_hbm.1, bf16[256,240]{1,0:T(8,128)(2,1)} %constant.12.clone.pack_hbm, f32[40,2560]{1,0:T(8,128)} %coef_hbm.1, ...), custom_call_target="tpu_custom_call" | custom-call | tf_op jit(solution)/shard_map/whole/pallas_call | solution.py:480
  101.5 2.2 %copy.18 = bf16[4,6,16,1280]{3,2,1,0:T(8,128)(2,1)} copy(bf16[4,6,16,1280]{3,2,1,0:T(8,128)(2,1)} %whole.1) | data formatting | bytes 1966080

commit v3 on v2

--- a/solution.py
+++ b/solution.py
@@ -14,6 +14,7 @@
 LEVS = 8
 DEVS = 256
 CYC = 5
+HALF = DEVS * 8
 SECTIONS = ((0, 0, 0, 96), (0, 1, 96, 128), (1, 1, 0, 64), (1, 2, 64, 128), (2, 2, 0, 32), (2, 3, 32, 128))
 
 
@@ -26,17 +27,16 @@
 
 
 def constant_arrays():
-    block, row = np.divmod(np.arange(256), 16)
+    half, rest = np.divmod(np.arange(256), 128)
+    block, row = np.divmod(rest, 8)
+    row = row + half * 8
     tile, cyc = np.divmod(np.arange(240), 80)
-    pack = (row[:, None] < 15) & (row[:, None] // 5 == tile[None]) & (5 * block[:, None] + row[:, None] % 5 == cyc[None])
-    src_u, rest = np.divmod(np.arange(480), 96)
-    src_t, src_w = np.divmod(rest, 32)
-    in_w, in_row = np.divmod(np.arange(512), 16)
-    unpack = (src_w[:, None] == in_w[None]) & (src_t[:, None] * 5 + src_u[:, None] == in_row[None])
+    pack = (row[:, None] < 15) & (row[:, None] % 3 == tile[None]) & (5 * block[:, None] + row[:, None] // 3 == cyc[None])
+    out_row, out_w = np.divmod(np.arange(256), 32)
+    in_w, in_row = np.divmod(np.arange(256), 8)
+    unpack = (out_w[:, None] == in_w[None]) & (out_row[:, None] == in_row[None])
     spread = np.arange(96)[:, None] == np.arange(384)[None] % 96
-    fu, dest = np.divmod(np.arange(240), 16)
-    back = (block[:, None] == dest[None]) & (row[:, None] == fu[None])
-    return [x.astype(np.float32) for x in (pack, unpack, spread, back, pack.T, np.eye(256))]
+    return [x.astype(np.float32) for x in (pack, unpack, spread, unpack.T, pack.T, np.eye(256))]
 
 
 def position():
@@ -85,8 +85,10 @@
         rows = pl.ds(pl.multiple_of(g * 80, 16), 80)
         x = jnp.concatenate([waves_out[t, rows, :] for t in range(3)], axis=0)
         y = nn_dot(pack[...], x).astype(BF)
-        send[pl.ds(g * 16, 16)] = y[:, :128].reshape(16, 16, 128)
-        send[pl.ds(128 + g * 16, 16)] = y[:, 128:].reshape(16, 16, 128)
+        for half in range(2):
+            for side in range(2):
+                rows = pl.ds(pl.multiple_of(half * HALF + side * 1024 + g * 128, 128), 128)
+                send[rows, :] = y[half * 128 : half * 128 + 128, side * 128 : side * 128 + 128]
         return 0
 
     lax.fori_loop(0, 8, block, 0)
@@ -133,21 +135,25 @@
         table[u, 128:256, cols] = (-(sl * ca + cl * sa)).astype(BF)
 
 
-def gather_waves(recv, unpack, spread, wave_row, fields):
+def gather_waves(half, recv, unpack, spread, wave_row, split, fields):
     lane = lax.broadcasted_iota(jnp.int32, (1, 384), 1)
     sections = [jnp.where((lane >= 96 * m) & (lane < 96 * m + 96), 1.0, 0.0).astype(BF) for m in range(4)]
     factor = jnp.where(wave_row[0:1, :] == 0.0, 1.0, 2.0)
 
     def pair(sp, _):
-        first = recv[pl.ds(sp * 64, 32)].reshape(512, 128)
-        second = recv[pl.ds(sp * 64 + 32, 32)].reshape(512, 128)
+        first = recv[pl.ds(pl.multiple_of(half * HALF + sp * 512, 256), 256), :]
+        second = recv[pl.ds(pl.multiple_of(half * HALF + sp * 512 + 256, 256), 256), :]
         z = nn_dot(unpack[...], jnp.concatenate([first, second], axis=1)).astype(BF)
-        for u in range(CYC):
+        if half == 0:
+            split[sp] = z[192:256]
+            rows_of = {u: [z[96 * u + 32 * t : 96 * u + 32 * t + 32] for t in range(3)] for u in (0, 1)}
+        else:
+            rows_of = {u: [z[96 * u - 256 + 32 * t : 96 * u - 224 + 32 * t] for t in range(3)] for u in (3, 4)}
+            rows_of[2] = [split[sp, 0:32], split[sp, 32:64], z[0:32]]
+        for u, tiles in rows_of.items():
             pieces = []
             for h in range(2):
-                zu = jnp.concatenate(
-                    [z[u * 96 + t * 32 : u * 96 + t * 32 + 32, h * 128 : h * 128 + 128] for t in range(3)], axis=1
-                )
+                zu = jnp.concatenate([x[:, h * 128 : h * 128 + 128] for x in tiles], axis=1)
                 pieces += [zu * sections[m] for m in range(4)]
             y = nt_dot(spread[...], jnp.concatenate(pieces, axis=0))
             for h in range(2):
@@ -176,30 +182,39 @@
     analysed[u] = (total / count).astype(BF)
 
 
-def pack_return(back, analysed, send):
+def pack_return(half, back, analysed, send):
+    places = [divmod(half * 8 + i, 3) for i in range(8)]
+
     def pair(g, _):
-        halves = []
+        groups = []
         for h in range(2):
-            rows = pl.ds(pl.multiple_of(g * 32 + h * 16, 16), 16)
-            halves.append(
+            rows = pl.ds(pl.multiple_of(g * 64 + h * 32, 32), 32)
+            groups.append(
                 jnp.concatenate(
-                    [analysed[u, rows, f * 128 : f * 128 + 128] for f in range(3) for u in range(CYC)], axis=0
+                    [
+                        analysed[u, rows, f * 128 : f * 128 + 128] if u < CYC else jnp.zeros((32, 128), BF)
+                        for u, f in places
+                    ],
+                    axis=0,
                 )
             )
-        y = nn_dot(back[...], jnp.concatenate(halves, axis=1)).astype(BF)
-        send[pl.ds(g * 32, 16)] = y[:, :128].reshape(16, 16, 128)
-        send[pl.ds(g * 32 + 16, 16)] = y[:, 128:].reshape(16, 16, 128)
-        return 0
-
-    lax.fori_loop(0, 8, pair, 0)
+        y = nn_dot(back[...], jnp.concatenate(groups, axis=1)).astype(BF)
+        for h in range(2):
+            rows = pl.ds(pl.multiple_of(half * HALF + g * 512 + h * 256, 256), 256)
+            send[rows, :] = y[:, h * 128 : h * 128 + 128]
+        return 0
+
+    lax.fori_loop(0, 4, pair, 0)
 
 
 def parity_parts(recv, packt, weight_col, parts):
     def block(g, _):
         rows = pl.ds(pl.multiple_of(g * 80, 16), 80)
-        x = jnp.concatenate(
-            [recv[pl.ds(g * 16, 16)].reshape(256, 128), recv[pl.ds(128 + g * 16, 16)].reshape(256, 128)], axis=1
-        )
+        sides = []
+        for side in range(2):
+            starts = [pl.multiple_of(half * HALF + side * 1024 + g * 128, 128) for half in range(2)]
+            sides.append(jnp.concatenate([recv[pl.ds(x, 128), :] for x in starts], axis=0))
+        x = jnp.concatenate(sides, axis=1)
         z = nn_dot(packt[...], x)
         weight = weight_col[rows, :]
         for f in range(3):
@@ -212,7 +227,7 @@
     lax.fori_loop(0, 8, block, 0)
 
 
-def forward_modes(leg_m, length, wave, eye, parts, flipped, modes_in, modes_out, depth_col, update):
+def forward_modes(leg_m, length, wave, eye, parts, flipped, modes_in, modes_out, depth_col, update, ready):
     for f in range(3):
         t = nt_dot(eye[...], parts[f]).astype(BF)
         flipped[0, f * 128 : f * 128 + 128, :] = t[:128]
@@ -234,16 +249,24 @@
             vals = nn_dot(modes_in[...], proj[f * 128 : f * 128 + 128])
             scaled = (vals * damp).astype(BF)
             update[f, :, cols] = nn_dot(modes_out[...], scaled).astype(BF)
+        if ready is not None:
+
+            @pl.when(ic > 0)
+            def _():
+                ready(ic - 1)
+
         return 0
 
     lax.fori_loop(0, NT // 256, block, 0)
+    if ready is not None:
+        ready(NT // 256 - 1)
 
 
 def column_of(row):
     return jnp.transpose(jnp.broadcast_to(row, (128, 128)))
 
 
-def side_columns(waves_row, weights_row, depths_row, wave_col, wave_row, weight_col, depth_col):
+def side_columns(waves_row, weights, depths_row, wave_col, wave_row, weight_col, depth_col):
     place = lax.broadcasted_iota(jnp.int32, (128, 128), 0)
     slot = lax.broadcasted_iota(jnp.int32, (128, 128), 1)
     order = jnp.where((place % 32) * 4 + place // 32 == slot, 1.0, 0.0).astype(BF)
@@ -254,22 +277,26 @@
     wave_col[...] = column
     wave_row[...] = jnp.transpose(column)[0:8]
     for i in range(5):
-        weight_col[i * 128 : i * 128 + 128, :] = column_of(weights_row[:, i * 128 : i * 128 + 128])
+        weight_col[i * 128 : i * 128 + 128, :] = column_of(weights[i : i + 1, :])
     depth_col[...] = column_of(depths_row[...])
 
 
-def send_all(send, recv, send_sem, recv_sem, own_sem, source_slot, my_slot):
+def send_half(half, send, recv, sems, source_slot, my_slot):
     w, s = position()
-    pltpu.make_async_copy(send.at[source_slot(w, s)], recv.at[my_slot], own_sem).start()
+
+    def rows(slot):
+        return pl.ds(pl.multiple_of(half * HALF + slot * 8, 8), 8)
+
+    pltpu.make_async_copy(send.at[rows(source_slot(w, s))], recv.at[rows(my_slot)], sems.at[half, 0]).start()
 
     def start(i, _):
         tw = lax.rem(w + lax.rem(i, WAVES), WAVES)
         ts = lax.rem(s + i // WAVES, LEVS)
         pltpu.make_async_remote_copy(
-            src_ref=send.at[source_slot(tw, ts)],
-            dst_ref=recv.at[my_slot],
-            send_sem=send_sem,
-            recv_sem=recv_sem,
+            src_ref=send.at[rows(source_slot(tw, ts))],
+            dst_ref=recv.at[rows(my_slot)],
+            send_sem=sems.at[half, 1],
+            recv_sem=sems.at[half, 2],
             device_id=(tw, ts),
             device_id_type=MESH,
         ).start()
@@ -278,11 +305,16 @@
     lax.fori_loop(1, DEVS, start, 0)
 
 
-def wait_all(send, recv, send_sem, recv_sem, own_sem):
-    rest = pl.ds(0, DEVS - 1)
-    pltpu.make_async_copy(send.at[0], recv.at[0], own_sem).wait()
-    pltpu.make_async_copy(send.at[rest], send.at[rest], send_sem).wait()
-    pltpu.make_async_copy(recv.at[rest], recv.at[rest], recv_sem).wait()
+def wait_half(half, send, recv, sems):
+    rest = pl.ds(half * HALF, HALF - 8)
+    block = pl.ds(half * HALF, 8)
+    pltpu.make_async_copy(send.at[block], recv.at[block], sems.at[half, 0]).wait()
+    pltpu.make_async_copy(recv.at[rest], recv.at[rest], sems.at[half, 2]).wait()
+
+
+def wait_sent(half, send, sems):
+    rest = pl.ds(half * HALF, HALF - 8)
+    pltpu.make_async_copy(send.at[rest], send.at[rest], sems.at[half, 1]).wait()
 
 
 def signal_peers(sem, peers):
@@ -293,7 +325,7 @@
 LEV_PEERS = [(0, 0, dx, dc) for dx in range(4) for dc in range(2) if dx or dc]
 Y_PEERS = [(0, dy, 0, 0) for dy in range(1, 4)]
 Z_PEERS = [(dz, 0, 0, 0) for dz in range(1, 8)]
-N_LATE = 6
+N_LATE = 11
 
 
 def whole(
@@ -309,8 +341,8 @@
     back_hbm,
     packt_hbm,
     eye_hbm,
+    weights_hbm,
     waves_row,
-    weights_row,
     depths_row,
     modes_in,
     modes_out,
@@ -328,6 +360,7 @@
     waves_out,
     send_a,
     recv_a,
+    split,
     table,
     low,
     fields,
@@ -342,6 +375,7 @@
     wave_row,
     weight_col,
     depth_col,
+    weights,
     load_sem,
     late_sem,
     y_sem,
@@ -368,6 +402,7 @@
                 (back_hbm, back),
                 (packt_hbm, packt),
                 (eye_hbm, eye),
+                *[(weights_hbm.at[pl.ds(i * 128, 128)], weights.at[i]) for i in range(5)],
             ]
         )
     ]
@@ -392,10 +427,12 @@
     inverse_pack(pack, waves_out, send_a)
     pl.semaphore_wait(z_sem, len(Z_PEERS))
 
-    a_sems = [sems_a.at[i] for i in range(3)]
-    send_all(send_a, recv_a, *a_sems, lambda tw, ts: mirrored(tw * LEVS + ts), s * WAVES + w)
-
-    side_columns(waves_row, weights_row, depths_row, wave_col, wave_row, weight_col, depth_col)
+    for half in range(2):
+        send_half(half, send_a, recv_a, sems_a, lambda tw, ts: mirrored(tw * LEVS + ts), s * WAVES + w)
+
+    for copy in late:
+        copy.wait()
+    side_columns(waves_row, weights, depths_row, wave_col, wave_row, weight_col, depth_col)
 
     def shift(u):
         return jnp.where(dest < 128, u, 4 - u)
@@ -405,24 +442,55 @@
         return 0
 
     lax.fori_loop(0, CYC, make_table, 0)
-    for copy in late:
-        copy.wait()
-    wait_all(send_a, recv_a, *a_sems)
-
-    gather_waves(recv_a, unpack, spread, wave_row, fields)
 
     def cycle(u, _):
         points = cyc[dest * CYC + shift(u)]
         grid_cycle(u, points, coef[pl.ds(s * CYC + shift(u), 1), :], table, fields, tend, analysed)
         return 0
 
-    lax.fori_loop(0, CYC, cycle, 0)
-    pack_return(back, analysed, send_b)
-    b_sems = [sems_b.at[i] for i in range(3)]
-    send_all(
-        send_b, recv_b, *b_sems, lambda tw, ts: lax.rem(ts, 2) * 128 + (ts // 2) * 32 + tw, mirrored(w * LEVS + s)
-    )
-    wait_all(send_b, recv_b, *b_sems)
+    def return_half(half):
+        pack_return(half, back, analysed, send_b)
+        send_half(
+            half,
+            send_b,
+            recv_b,
+            sems_b,
+            lambda tw, ts: lax.rem(ts, 2) * 128 + (ts // 2) * 32 + tw,
+            mirrored(w * LEVS + s),
+        )
+
+    wait_half(0, send_a, recv_a, sems_a)
+    gather_waves(0, recv_a, unpack, spread, wave_row, split, fields)
+    lax.fori_loop(0, 2, cycle, 0)
+    wait_half(1, send_a, recv_a, sems_a)
+    gather_waves(1, recv_a, unpack, spread, wave_row, split, fields)
+    cycle(2, 0)
+    return_half(0)
+    lax.fori_loop(3, CYC, cycle, 0)
+    return_half(1)
+    for half in range(2):
+        wait_sent(half, send_a, sems_a)
+        wait_half(half, send_b, recv_b, sems_b)
+        wait_sent(half, send_b, sems_b)
+
+    def to_levels(ic):
+        cols = pl.ds(pl.multiple_of(ic * 256, 256), 256)
+        place = out.at[m, pl.ds(r * 3, 3), :, cols]
+
+        def piece(ts):
+            return update.at[:, pl.ds(pl.multiple_of(ts * 16, 16), 16), cols]
+
+        for i in range(1, LEVS):
+            ts = lax.rem(s + i, LEVS)
+            pltpu.make_async_remote_copy(
+                src_ref=piece(ts),
+                dst_ref=place,
+                send_sem=sems_c.at[0],
+                recv_sem=sems_c.at[1],
+                device_id=(w, ts),
+                device_id_type=MESH,
+            ).start()
+        pltpu.make_async_copy(piece(s), place, sems_c.at[1]).start()
 
     parity_parts(recv_b, packt, weight_col, parts)
     forward_modes(
@@ -436,23 +504,8 @@
         modes_out,
         depth_col,
         update,
+        to_levels,
     )
-
-    def piece(ts):
-        return update.at[:, pl.ds(pl.multiple_of(ts * 16, 16), 16), :]
-
-    place = out.at[m, pl.ds(r * 3, 3)]
-    for i in range(1, LEVS):
-        ts = lax.rem(s + i, LEVS)
-        pltpu.make_async_remote_copy(
-            src_ref=piece(ts),
-            dst_ref=place,
-            send_sem=sems_c.at[0],
-            recv_sem=sems_c.at[1],
-            device_id=(w, ts),
-            device_id_type=MESH,
-        ).start()
-    pltpu.make_async_copy(piece(s), place, sems_c.at[1]).start()
     sent = update.at[:, 0:112, :]
     pltpu.make_async_copy(sent, sent, sems_c.at[0]).wait()
     pltpu.make_async_copy(out, out, sems_c.at[1]).wait()
@@ -479,30 +532,31 @@
     vmem = pltpu.VMEM
     return pl.pallas_call(
         whole,
-        out_shape=jax.ShapeDtypeStruct((4, 6, 16, NT), BF),
-        in_specs=[SM] * 3 + [ANY] * 9 + [VM] * 5,
-        out_specs=ANY,
+        out_shape=pltpu.VMEM((4, 6, 16, NT), BF),
+        in_specs=[SM] * 3 + [ANY] * 10 + [VM] * 4,
+        out_specs=VM,
         scratch_shapes=[
             vmem((384, NT), BF),
             vmem((4, 640, NT), BF),
             vmem((256, 240), BF),
             vmem((40, 2560), F32),
-            vmem((480, 512), BF),
+            vmem((256, 256), BF),
             vmem((96, 384), BF),
-            vmem((256, 240), BF),
+            vmem((256, 256), BF),
             vmem((240, 256), BF),
             vmem((256, 256), BF),
             vmem((6, 256, NT), BF),
             vmem((3, 640, 256), BF),
-            vmem((DEVS, 16, 128), BF),
-            vmem((DEVS, 16, 128), BF),
+            vmem((2 * HALF, 128), BF),
+            vmem((2 * HALF, 128), BF),
+            vmem((4, 64, 256), BF),
             vmem((CYC, 256, 2560), BF),
             vmem((2, 128, 256), F32),
             vmem((CYC, 384, 256), BF),
             vmem((384, 2560), BF),
             vmem((CYC, 256, 384), BF),
-            vmem((DEVS, 16, 128), BF),
-            vmem((DEVS, 16, 128), BF),
+            vmem((2 * HALF, 128), BF),
+            vmem((2 * HALF, 128), BF),
             vmem((3, 640, 256), BF),
             vmem((2, 384, 640), BF),
             vmem((3, 128, NT), BF),
@@ -510,12 +564,13 @@
             vmem((8, 128), F32),
             vmem((640, 128), F32),
             vmem((128, 128), F32),
+            vmem((8, 128), F32),
             pltpu.SemaphoreType.DMA((6,)),
             pltpu.SemaphoreType.DMA((N_LATE,)),
             pltpu.SemaphoreType.REGULAR,
             pltpu.SemaphoreType.REGULAR,
-            pltpu.SemaphoreType.DMA((3,)),
-            pltpu.SemaphoreType.DMA((3,)),
+            pltpu.SemaphoreType.DMA((2, 3)),
+            pltpu.SemaphoreType.DMA((2, 3)),
             pltpu.SemaphoreType.DMA((2,)),
         ],
         name="whole",
@@ -535,8 +590,8 @@
         back,
         packt,
         eye,
+        cycle_weights,
         wave_ids.reshape(1, 128),
-        cycle_weights.reshape(1, 640),
         depths.reshape(1, 128),
         modes_in,
         modes_out,

time: 104 us -> 93 us (0.89)
  Pallas kernels: 100 us -> 91.9 us
  local copies, waits for them, and re-layouts: 3.48 us -> 0.95 us
    pallas_call x1, Pallas kernels: 100 us -> 91.9 us  [on_device(): pl.pallas_call(whole, out_shape=pltpu.VMEM((4, 6, 16, NT), BF), in_specs=...]
    reshape x1 -> x0, local copies, waits for them, and re-layouts: 1.27 us -> none  [on_device(): cycle_weights.reshape(1, 640)]
    unnamed x1, local copies, waits for them, and re-layouts: 2.21 us -> 0.95 us
where the time goes in v3:
time: 93 us; the launch traced here: 92.8 us
  Pallas kernels  91.9 us (99%)
  local copies, waits for them, and re-layouts  0.95 us (1%)
    pallas_call x1, Pallas kernels, on_device(): pl.pallas_call(whole, out_shape=pltpu.VMEM((4, 6, 16, NT), BF), in_specs=...  91.9 us

profile of v3, /device:TPU:1, one launch (start us, length us, event | category | flops | bytes accessed | tf_op | source)
XLA Modules:
  0.0 92.8 jit_solution(10241360631551133228)
XLA Ops:
  0.0 91.9 %whole.1 = bf16[4,6,16,1280]{3,2,1,0:T(8,128)(2,1)S(1)} custom-call(s32[128]{0:T(128)} %lens.1, s32[128]{0:T(128)} %waves.1, s32[1280]{0:T(1024)} %cyc.1, bf16[384,1280]{1,0:T(8,128)(2,1)} %bitcast.3, bf16[4,640,1280]{2,1,0:T(8,128)(2,1)} %leg_hbm.1, bf16[256,240]{1,0:T(8,128)(2,1)} %constant.12.clone.pack_hbm, f32[40,2560]{1,0:T(8,128)} %coef_hbm.1, ...), custom_call_target="tpu_custom_call" | custom-call | tf_op jit(solution)/shard_map/whole/pallas_call | solution.py:533
  91.9 0.9 %copy.18 = bf16[4,6,16,1280]{3,2,1,0:T(8,128)(2,1)} copy(bf16[4,6,16,1280]{3,2,1,0:T(8,128)(2,1)S(1)} %whole.1) | data formatting | bytes 1966080

commit v4 on v3

--- a/solution.py
+++ b/solution.py
@@ -91,7 +91,7 @@
                 send[rows, :] = y[half * 128 : half * 128 + 128, side * 128 : side * 128 + 128]
         return 0
 
-    lax.fori_loop(0, 8, block, 0)
+    lax.fori_loop(0, 8, block, 0, unroll=4)
 
 
 def cos_sin(steps, count):
@@ -135,21 +135,26 @@
         table[u, 128:256, cols] = (-(sl * ca + cl * sa)).astype(BF)
 
 
-def gather_waves(half, recv, unpack, spread, wave_row, split, fields):
+def gather_waves(cycles, recv, unpack, spread, wave_row, split, fields):
     lane = lax.broadcasted_iota(jnp.int32, (1, 384), 1)
     sections = [jnp.where((lane >= 96 * m) & (lane < 96 * m + 96), 1.0, 0.0).astype(BF) for m in range(4)]
     factor = jnp.where(wave_row[0:1, :] == 0.0, 1.0, 2.0)
 
     def pair(sp, _):
-        first = recv[pl.ds(pl.multiple_of(half * HALF + sp * 512, 256), 256), :]
-        second = recv[pl.ds(pl.multiple_of(half * HALF + sp * 512 + 256, 256), 256), :]
-        z = nn_dot(unpack[...], jnp.concatenate([first, second], axis=1)).astype(BF)
-        if half == 0:
-            split[sp] = z[192:256]
-            rows_of = {u: [z[96 * u + 32 * t : 96 * u + 32 * t + 32] for t in range(3)] for u in (0, 1)}
+        def sorted_half(half):
+            starts = [pl.multiple_of(half * HALF + sp * 512 + h * 256, 256) for h in range(2)]
+            return nn_dot(unpack[...], jnp.concatenate([recv[pl.ds(x, 256), :] for x in starts], axis=1)).astype(BF)
+
+        if cycles == (0, 1):
+            z = sorted_half(0)
+            split[sp, 0:64] = z[192:256]
+            rows_of = {u: [z[96 * u + 32 * t : 96 * u + 32 * t + 32] for t in range(3)] for u in cycles}
+        elif cycles == (2,):
+            z = sorted_half(1)
+            split[sp, 64:256] = z[32:224]
+            rows_of = {2: [split[sp, 0:32], split[sp, 32:64], z[0:32]]}
         else:
-            rows_of = {u: [z[96 * u - 256 + 32 * t : 96 * u - 224 + 32 * t] for t in range(3)] for u in (3, 4)}
-            rows_of[2] = [split[sp, 0:32], split[sp, 32:64], z[0:32]]
+            rows_of = {u: [split[sp, 96 * u - 224 + 32 * t : 96 * u - 192 + 32 * t] for t in range(3)] for u in cycles}
         for u, tiles in rows_of.items():
             pieces = []
             for h in range(2):
@@ -164,7 +169,7 @@
                         fields[u, rows, r * 128 : r * 128 + 128] = part[r * 48 + f * 16 : r * 48 + f * 16 + 16, :]
         return 0
 
-    lax.fori_loop(0, 4, pair, 0)
+    lax.fori_loop(0, 4, pair, 0, unroll=2)
 
 
 def grid_cycle(u, points, coef_row, table, fields, tend, analysed):
@@ -178,8 +183,8 @@
                 g[f * 128 : f * 128 + 128] * (coef + g[nxt * 128 : nxt * 128 + 128])
             ).astype(BF)
     total = nt_dot(table[u], tend[...])
-    count = jnp.full((1, 384), points, jnp.int32).astype(F32)
-    analysed[u] = (total / count).astype(BF)
+    share = 1.0 / jnp.full((1, 384), points, jnp.int32).astype(F32)
+    analysed[u] = (total * share).astype(BF)
 
 
 def pack_return(half, back, analysed, send):
@@ -204,7 +209,7 @@
             send[rows, :] = y[:, h * 128 : h * 128 + 128]
         return 0
 
-    lax.fori_loop(0, 4, pair, 0)
+    lax.fori_loop(0, 4, pair, 0, unroll=2)
 
 
 def parity_parts(recv, packt, weight_col, parts):
@@ -224,42 +229,37 @@
             parts[f, rows, 128:256] = (weight * (north - south)).astype(BF)
         return 0
 
-    lax.fori_loop(0, 8, block, 0)
-
-
-def forward_modes(leg_m, length, wave, eye, parts, flipped, modes_in, modes_out, depth_col, update, ready):
+    lax.fori_loop(0, 8, block, 0, unroll=4)
+
+
+def make_damp(wave, depth_col, damp):
+    for a in range(NT // 128):
+        degree = (lax.broadcasted_iota(jnp.int32, (1, 128), 1) + (wave + a * 128)).astype(F32)
+        damp[:, a * 128 : a * 128 + 128] = 1.0 / (1.0 + depth_col[...] * degree * (degree + 1.0) / float(NT * NT))
+
+
+def forward_modes(leg_m, length, eye, parts, flipped, modes_in, modes_out, damp, update, ready):
     for f in range(3):
         t = nt_dot(eye[...], parts[f]).astype(BF)
-        flipped[0, f * 128 : f * 128 + 128, :] = t[:128]
-        flipped[1, f * 128 : f * 128 + 128, :] = t[128:]
+        flipped[f * 128 : f * 128 + 128, :] = t[:128]
+        flipped[384 + f * 128 : 512 + f * 128, :] = t[128:]
     lane = lax.broadcasted_iota(jnp.int32, (1, 256), 1)
     even_lane = lane % 2 == 0
 
     def block(ic, _):
         cols = pl.ds(pl.multiple_of(ic * 256, 256), 256)
-        polys = leg_m(cols)
-        even = nn_dot(flipped[0], polys)
-        odd = nn_dot(flipped[1], polys)
-        where = lane + ic * 256
-        proj = jnp.where(where < length, jnp.where(even_lane, even, odd), 0.0).astype(BF)
-        degree = (where + wave).astype(F32)
-        depth = depth_col[:, 0:1]
-        damp = 1.0 / (1.0 + depth * degree * (degree + 1.0) / float(NT * NT))
+        both = nn_dot(flipped[...], leg_m(cols))
+        live = lane + ic * 256 < length
         for f in range(3):
-            vals = nn_dot(modes_in[...], proj[f * 128 : f * 128 + 128])
-            scaled = (vals * damp).astype(BF)
+            even = both[f * 128 : f * 128 + 128]
+            odd = both[384 + f * 128 : 512 + f * 128]
+            proj = jnp.where(live, jnp.where(even_lane, even, odd), 0.0).astype(BF)
+            scaled = (nn_dot(modes_in[...], proj) * damp[:, cols]).astype(BF)
             update[f, :, cols] = nn_dot(modes_out[...], scaled).astype(BF)
-        if ready is not None:
-
-            @pl.when(ic > 0)
-            def _():
-                ready(ic - 1)
-
+        ready(ic)
         return 0
 
     lax.fori_loop(0, NT // 256, block, 0)
-    if ready is not None:
-        ready(NT // 256 - 1)
 
 
 def column_of(row):
@@ -322,16 +322,15 @@
         pl.semaphore_signal(sem, inc=1, device_id=shifted(*peer), device_id_type=MESH)
 
 
-LEV_PEERS = [(0, 0, dx, dc) for dx in range(4) for dc in range(2) if dx or dc]
-Y_PEERS = [(0, dy, 0, 0) for dy in range(1, 4)]
+PLANE_PEERS = [(0, dy, dx, dc) for dx in range(4) for dy in range(4) for dc in range(2) if dx or dy or dc]
 Z_PEERS = [(dz, 0, 0, 0) for dz in range(1, 8)]
-N_LATE = 11
+N_LATE = 17
 
 
 def whole(
-    lens,
-    waves,
-    cyc,
+    lens_hbm,
+    waves_hbm,
+    cyc_hbm,
     spec_hbm,
     leg_hbm,
     pack_hbm,
@@ -342,11 +341,19 @@
     packt_hbm,
     eye_hbm,
     weights_hbm,
+    waves_row_hbm,
+    depths_row_hbm,
+    modes_in_hbm,
+    modes_out_hbm,
+    out,
+    lens,
+    waves,
+    cyc,
     waves_row,
     depths_row,
     modes_in,
     modes_out,
-    out,
+    damp,
     spec,
     leg,
     pack,
@@ -378,7 +385,6 @@
     weights,
     load_sem,
     late_sem,
-    y_sem,
     z_sem,
     sems_a,
     sems_b,
@@ -391,7 +397,7 @@
 
     loads = [pltpu.make_async_copy(spec_hbm, spec, load_sem.at[0])]
     loads += [pltpu.make_async_copy(leg_hbm.at[i], leg.at[i], load_sem.at[1 + i]) for i in range(4)]
-    loads += [pltpu.make_async_copy(pack_hbm, pack, load_sem.at[5])]
+    loads += [pltpu.make_async_copy(pack_hbm, pack, load_sem.at[5]), pltpu.make_async_copy(lens_hbm, lens, load_sem.at[6])]
     late = [
         pltpu.make_async_copy(a, b, late_sem.at[i])
         for i, (a, b) in enumerate(
@@ -402,25 +408,30 @@
                 (back_hbm, back),
                 (packt_hbm, packt),
                 (eye_hbm, eye),
+                (waves_hbm, waves),
+                (cyc_hbm, cyc),
+                (waves_row_hbm, waves_row),
+                (depths_row_hbm, depths_row),
+                (modes_in_hbm, modes_in),
+                (modes_out_hbm, modes_out),
                 *[(weights_hbm.at[pl.ds(i * 128, 128)], weights.at[i]) for i in range(5)],
             ]
         )
     ]
-    for copy in loads + late:
+    for copy in [loads[6]] + loads[:6] + late:
         copy.start()
 
-    signal_peers(barrier, LEV_PEERS + Y_PEERS + Z_PEERS)
+    signal_peers(barrier, Z_PEERS + PLANE_PEERS)
+    loads[6].wait()
     loads[0].wait()
     inverse_rows(spec, lambda i: lens[w * 4 + i], rhs)
     loads[1].wait()
     loads[2].wait()
     inverse_dots(0, leg, rhs, waves_out)
-    pl.semaphore_wait(barrier, len(LEV_PEERS + Y_PEERS + Z_PEERS))
-    signal_peers(y_sem, Y_PEERS)
+    pl.semaphore_wait(barrier, len(Z_PEERS + PLANE_PEERS))
+    signal_peers(z_sem, Z_PEERS)
     loads[3].wait()
     inverse_dots(1, leg, rhs, waves_out)
-    pl.semaphore_wait(y_sem, len(Y_PEERS))
-    signal_peers(z_sem, Z_PEERS)
     loads[4].wait()
     inverse_dots(2, leg, rhs, waves_out)
     loads[5].wait()
@@ -460,14 +471,16 @@
         )
 
     wait_half(0, send_a, recv_a, sems_a)
-    gather_waves(0, recv_a, unpack, spread, wave_row, split, fields)
+    gather_waves((0, 1), recv_a, unpack, spread, wave_row, split, fields)
     lax.fori_loop(0, 2, cycle, 0)
     wait_half(1, send_a, recv_a, sems_a)
-    gather_waves(1, recv_a, unpack, spread, wave_row, split, fields)
+    gather_waves((2,), recv_a, unpack, spread, wave_row, split, fields)
     cycle(2, 0)
     return_half(0)
+    gather_waves((3, 4), recv_a, unpack, spread, wave_row, split, fields)
     lax.fori_loop(3, CYC, cycle, 0)
     return_half(1)
+    make_damp(waves[w * 4 + m], depth_col, damp)
     for half in range(2):
         wait_sent(half, send_a, sems_a)
         wait_half(half, send_b, recv_b, sems_b)
@@ -496,13 +509,12 @@
     forward_modes(
         lambda cols: leg[m, :, cols],
         lens[w * 4 + m],
-        waves[w * 4 + m],
         eye,
         parts,
         flipped,
         modes_in,
         modes_out,
-        depth_col,
+        damp,
         update,
         to_levels,
     )
@@ -533,9 +545,17 @@
     return pl.pallas_call(
         whole,
         out_shape=pltpu.VMEM((4, 6, 16, NT), BF),
-        in_specs=[SM] * 3 + [ANY] * 10 + [VM] * 4,
+        in_specs=[ANY] * 17,
         out_specs=VM,
         scratch_shapes=[
+            pltpu.SMEM((128,), jnp.int32),
+            pltpu.SMEM((128,), jnp.int32),
+            pltpu.SMEM((NT,), jnp.int32),
+            vmem((1, 128), jnp.int32),
+            vmem((1, 128), F32),
+            vmem((128, 128), BF),
+            vmem((128, 128), BF),
+            vmem((128, NT), F32),
             vmem((384, NT), BF),
             vmem((4, 640, NT), BF),
             vmem((256, 240), BF),
@@ -549,7 +569,7 @@
             vmem((3, 640, 256), BF),
             vmem((2 * HALF, 128), BF),
             vmem((2 * HALF, 128), BF),
-            vmem((4, 64, 256), BF),
+            vmem((4, 256, 256), BF),
             vmem((CYC, 256, 2560), BF),
             vmem((2, 128, 256), F32),
             vmem((CYC, 384, 256), BF),
@@ -558,16 +578,15 @@
             vmem((2 * HALF, 128), BF),
             vmem((2 * HALF, 128), BF),
             vmem((3, 640, 256), BF),
-            vmem((2, 384, 640), BF),
+            vmem((768, 640), BF),
             vmem((3, 128, NT), BF),
             vmem((128, 128), F32),
             vmem((8, 128), F32),
             vmem((640, 128), F32),
             vmem((128, 128), F32),
             vmem((8, 128), F32),
-            pltpu.SemaphoreType.DMA((6,)),
+            pltpu.SemaphoreType.DMA((7,)),
             pltpu.SemaphoreType.DMA((N_LATE,)),
-            pltpu.SemaphoreType.REGULAR,
             pltpu.SemaphoreType.REGULAR,
             pltpu.SemaphoreType.DMA((2, 3)),
             pltpu.SemaphoreType.DMA((2, 3)),

time: 93 us -> 88.2 us (0.948)
  Pallas kernels: 91.9 us -> 87.2 us
    pallas_call x1, Pallas kernels: 91.9 us -> 87.2 us  [on_device(): pl.pallas_call(whole, out_shape=pltpu.VMEM((4, 6, 16, NT), BF), in_specs=...]
where the time goes in v4:
time: 88.2 us; the launch traced here: 88.1 us
  Pallas kernels  87.2 us (99%)
  local copies, waits for them, and re-layouts  0.95 us (1%)
    pallas_call x1, Pallas kernels, on_device(): pl.pallas_call(whole, out_shape=pltpu.VMEM((4, 6, 16, NT), BF), in_specs=...  87.2 us

profile of v4, /device:TPU:1, one launch (start us, length us, event | category | flops | bytes accessed | tf_op | source)
XLA Modules:
  0.0 88.1 jit_solution(14966475241181233769)
XLA Ops:
  0.0 87.2 %whole.1 = bf16[4,6,16,1280]{3,2,1,0:T(8,128)(2,1)S(1)} custom-call(s32[128]{0:T(128)} %lens_hbm.1, s32[128]{0:T(128)} %waves_hbm.1, s32[1280]{0:T(1024)} %cyc_hbm.1, bf16[384,1280]{1,0:T(8,128)(2,1)} %bitcast.3, bf16[4,640,1280]{2,1,0:T(8,128)(2,1)} %leg_hbm.1, bf16[256,240]{1,0:T(8,128)(2,1)} %constant.12.clone.pack_hbm, f32[40,2560]{1,0:T(8,128)} %coef_hbm.1, ...), custom_call_target="tpu_custom_call" | custom-call | tf_op jit(solution)/shard_map/whole/pallas_call | solution.py:545
  87.2 0.9 %copy.18 = bf16[4,6,16,1280]{3,2,1,0:T(8,128)(2,1)} copy(bf16[4,6,16,1280]{3,2,1,0:T(8,128)(2,1)S(1)} %whole.1) | data formatting | bytes 1966080

commit v5 on v4

--- a/solution.py
+++ b/solution.py
@@ -14,6 +14,8 @@
 LEVS = 8
 DEVS = 256
 CYC = 5
+UNROLL = 4
+CHUNKS = ((0, 256), (256, 256), (512, 256), (768, 256), (1024, 256))
 HALF = DEVS * 8
 SECTIONS = ((0, 0, 0, 96), (0, 1, 96, 128), (1, 1, 0, 64), (1, 2, 64, 128), (2, 2, 0, 32), (2, 3, 32, 128))
 
@@ -246,20 +248,30 @@
     lane = lax.broadcasted_iota(jnp.int32, (1, 256), 1)
     even_lane = lane % 2 == 0
 
-    def block(ic, _):
-        cols = pl.ds(pl.multiple_of(ic * 256, 256), 256)
-        both = nn_dot(flipped[...], leg_m(cols))
-        live = lane + ic * 256 < length
+    def project(start, width):
+        both = nn_dot(flipped[...], leg_m(slice(start, start + width)))
+        live = lane[:, :width] + start < length
+        parts = []
         for f in range(3):
             even = both[f * 128 : f * 128 + 128]
             odd = both[384 + f * 128 : 512 + f * 128]
-            proj = jnp.where(live, jnp.where(even_lane, even, odd), 0.0).astype(BF)
-            scaled = (nn_dot(modes_in[...], proj) * damp[:, cols]).astype(BF)
-            update[f, :, cols] = nn_dot(modes_out[...], scaled).astype(BF)
-        ready(ic)
-        return 0
-
-    lax.fori_loop(0, NT // 256, block, 0)
+            parts.append(jnp.where(live, jnp.where(even_lane[:, :width], even, odd), 0.0).astype(BF))
+        return jnp.concatenate(parts, axis=1)
+
+    def mix(start, width, proj):
+        cols = slice(start, start + width)
+        vals = nn_dot(modes_in[...], proj)
+        scaled = (vals * jnp.concatenate([damp[:, cols]] * 3, axis=1)).astype(BF)
+        mixed = nn_dot(modes_out[...], scaled).astype(BF)
+        for f in range(3):
+            update[f, :, cols] = mixed[:, f * width : f * width + width]
+
+    proj = project(*CHUNKS[0])
+    for chunk, following in zip(CHUNKS, CHUNKS[1:] + (None,)):
+        after = project(*following) if following else None
+        mix(*chunk, proj)
+        ready(*chunk)
+        proj = after
 
 
 def column_of(row):
@@ -281,40 +293,49 @@
     depth_col[...] = column_of(depths_row[...])
 
 
-def send_half(half, send, recv, sems, source_slot, my_slot):
+def send_class(half, core, send, recv, spare, sems, source_slot, my_slot):
     w, s = position()
 
     def rows(slot):
         return pl.ds(pl.multiple_of(half * HALF + slot * 8, 8), 8)
 
-    pltpu.make_async_copy(send.at[rows(source_slot(w, s))], recv.at[rows(my_slot)], sems.at[half, 0]).start()
-
-    def start(i, _):
-        tw = lax.rem(w + lax.rem(i, WAVES), WAVES)
-        ts = lax.rem(s + i // WAVES, LEVS)
+    def start(tw, ts):
         pltpu.make_async_remote_copy(
             src_ref=send.at[rows(source_slot(tw, ts))],
             dst_ref=recv.at[rows(my_slot)],
-            send_sem=sems.at[half, 1],
+            send_sem=sems.at[half, core],
             recv_sem=sems.at[half, 2],
             device_id=(tw, ts),
             device_id_type=MESH,
         ).start()
-        return 0
-
-    lax.fori_loop(1, DEVS, start, 0)
-
-
-def wait_half(half, send, recv, sems):
-    rest = pl.ds(half * HALF, HALF - 8)
-    block = pl.ds(half * HALF, 8)
-    pltpu.make_async_copy(send.at[block], recv.at[block], sems.at[half, 0]).wait()
-    pltpu.make_async_copy(recv.at[rest], recv.at[rest], sems.at[half, 2]).wait()
-
-
-def wait_sent(half, send, sems):
-    rest = pl.ds(half * HALF, HALF - 8)
-    pltpu.make_async_copy(send.at[rest], send.at[rest], sems.at[half, 1]).wait()
+
+    for k in range(LEVS // 2):
+        ts = ((s // 2 + k) & 3) * 2 + core
+        if k == 0:
+            own = (s & 1) == core
+            pl.when(jnp.logical_not(own))(lambda ts=ts: start(w, ts))
+
+            @pl.when(own)
+            def _():
+                source = send.at[rows(source_slot(w, s))]
+                pltpu.make_async_copy(source, recv.at[rows(my_slot)], sems.at[half, 3]).start()
+                pltpu.make_async_copy(source, spare.at[half], sems.at[half, core]).start()
+
+        else:
+            start(w, ts)
+        lax.fori_loop(1, WAVES, lambda i, c, ts=ts: (start((w + i) & 31, ts), c)[1], 0, unroll=UNROLL)
+
+
+def wait_sent(half, core, send, sems):
+    part = send.at[pl.ds(half * HALF, HALF // 2)]
+    pltpu.make_async_copy(part, part, sems.at[half, core]).wait()
+
+
+def wait_half(half, recv, sems):
+    rest = recv.at[pl.ds(half * HALF, HALF - 8)]
+    own = recv.at[pl.ds(half * HALF, 8)]
+    pltpu.make_async_copy(own, own, sems.at[half, 3]).wait()
+    pltpu.make_async_copy(rest, rest, sems.at[half, 2]).wait()
 
 
 def signal_peers(sem, peers):
@@ -383,6 +404,8 @@
     weight_col,
     depth_col,
     weights,
+    spare_a,
+    spare_b,
     load_sem,
     late_sem,
     z_sem,
@@ -438,56 +461,65 @@
     inverse_pack(pack, waves_out, send_a)
     pl.semaphore_wait(z_sem, len(Z_PEERS))
 
-    for half in range(2):
-        send_half(half, send_a, recv_a, sems_a, lambda tw, ts: mirrored(tw * LEVS + ts), s * WAVES + w)
-
+    def to_cycles(half, core):
+        send_class(half, core, send_a, recv_a, spare_a, sems_a, lambda tw, ts: mirrored(tw * LEVS + ts), s * WAVES + w)
+
+    def to_waves(half, core):
+        send_class(
+            half,
+            core,
+            send_b,
+            recv_b,
+            spare_b,
+            sems_b,
+            lambda tw, ts: ((ts & 1) * 4 + (ts >> 1)) * 32 + tw,
+            mirrored(w * LEVS + s),
+        )
+
+    def shift(u):
+        return jnp.where(dest < 128, u, 4 - u)
+
+    def make_table(u, _):
+        cycle_table(u, wave_col, cyc[dest * CYC + shift(u)], table, low)
+        return 0
+
+    to_cycles(0, 0)
     for copy in late:
         copy.wait()
     side_columns(waves_row, weights, depths_row, wave_col, wave_row, weight_col, depth_col)
-
-    def shift(u):
-        return jnp.where(dest < 128, u, 4 - u)
-
-    def make_table(u, _):
-        cycle_table(u, wave_col, cyc[dest * CYC + shift(u)], table, low)
-        return 0
-
-    lax.fori_loop(0, CYC, make_table, 0)
+    make_table(0, 0)
+    to_cycles(1, 0)
+    lax.fori_loop(1, CYC, make_table, 0)
+    wait_sent(0, 0, send_a, sems_a)
+    to_cycles(0, 1)
+    to_cycles(1, 1)
 
     def cycle(u, _):
         points = cyc[dest * CYC + shift(u)]
         grid_cycle(u, points, coef[pl.ds(s * CYC + shift(u), 1), :], table, fields, tend, analysed)
         return 0
 
-    def return_half(half):
-        pack_return(half, back, analysed, send_b)
-        send_half(
-            half,
-            send_b,
-            recv_b,
-            sems_b,
-            lambda tw, ts: lax.rem(ts, 2) * 128 + (ts // 2) * 32 + tw,
-            mirrored(w * LEVS + s),
-        )
-
-    wait_half(0, send_a, recv_a, sems_a)
+    wait_half(0, recv_a, sems_a)
     gather_waves((0, 1), recv_a, unpack, spread, wave_row, split, fields)
     lax.fori_loop(0, 2, cycle, 0)
-    wait_half(1, send_a, recv_a, sems_a)
+    wait_half(1, recv_a, sems_a)
     gather_waves((2,), recv_a, unpack, spread, wave_row, split, fields)
     cycle(2, 0)
-    return_half(0)
+    pack_return(0, back, analysed, send_b)
+    to_waves(0, 0)
     gather_waves((3, 4), recv_a, unpack, spread, wave_row, split, fields)
+    pl.when((s & 1) == 0)(lambda: to_waves(0, 1))
     lax.fori_loop(3, CYC, cycle, 0)
-    return_half(1)
+    pack_return(1, back, analysed, send_b)
+    to_waves(1, 0)
+    pl.when((s & 1) == 1)(lambda: to_waves(0, 1))
     make_damp(waves[w * 4 + m], depth_col, damp)
+    to_waves(1, 1)
     for half in range(2):
-        wait_sent(half, send_a, sems_a)
-        wait_half(half, send_b, recv_b, sems_b)
-        wait_sent(half, send_b, sems_b)
-
-    def to_levels(ic):
-        cols = pl.ds(pl.multiple_of(ic * 256, 256), 256)
+        wait_half(half, recv_b, sems_b)
+
+    def to_levels(start, width):
+        cols = pl.ds(start, width)
         place = out.at[m, pl.ds(r * 3, 3), :, cols]
 
         def piece(ts):
@@ -518,6 +550,12 @@
         update,
         to_levels,
     )
+    for half in range(2):
+        wait_sent(half, 1, send_a, sems_a)
+        if half == 1:
+            wait_sent(1, 0, send_a, sems_a)
+        for core in range(2):
+            wait_sent(half, core, send_b, sems_b)
     sent = update.at[:, 0:112, :]
     pltpu.make_async_copy(sent, sent, sems_c.at[0]).wait()
     pltpu.make_async_copy(out, out, sems_c.at[1]).wait()
@@ -585,11 +623,13 @@
             vmem((640, 128), F32),
             vmem((128, 128), F32),
             vmem((8, 128), F32),
+            vmem((2, 8, 128), BF),
+            vmem((2, 8, 128), BF),
             pltpu.SemaphoreType.DMA((7,)),
             pltpu.SemaphoreType.DMA((N_LATE,)),
             pltpu.SemaphoreType.REGULAR,
-            pltpu.SemaphoreType.DMA((2, 3)),
-            pltpu.SemaphoreType.DMA((2, 3)),
+            pltpu.SemaphoreType.DMA((2, 4)),
+            pltpu.SemaphoreType.DMA((2, 4)),
             pltpu.SemaphoreType.DMA((2,)),
         ],
         name="whole",

time: 88.2 us -> 76.2 us (0.86)
  Pallas kernels: 87.2 us -> 75.2 us
    pallas_call x1, Pallas kernels: 87.2 us -> 75.2 us  [on_device(): pl.pallas_call(whole, out_shape=pltpu.VMEM((4, 6, 16, NT), BF), in_specs=...]
where the time goes in v5:
time: 76.2 us; the launch traced here: 76.1 us
  Pallas kernels  75.2 us (99%)
  local copies, waits for them, and re-layouts  0.95 us (1%)
    pallas_call x1, Pallas kernels, on_device(): pl.pallas_call(whole, out_shape=pltpu.VMEM((4, 6, 16, NT), BF), in_specs=...  75.2 us

profile of v5, /device:TPU:1, one launch (start us, length us, event | category | flops | bytes accessed | tf_op | source)
XLA Modules:
  0.0 76.1 jit_solution(8028312660432402171)
XLA Ops:
  0.0 75.2 %whole.1 = bf16[4,6,16,1280]{3,2,1,0:T(8,128)(2,1)S(1)} custom-call(s32[128]{0:T(128)} %lens_hbm.1, s32[128]{0:T(128)} %waves_hbm.1, s32[1280]{0:T(1024)} %cyc_hbm.1, bf16[384,1280]{1,0:T(8,128)(2,1)} %bitcast.3, bf16[4,640,1280]{2,1,0:T(8,128)(2,1)} %leg_hbm.1, bf16[256,240]{1,0:T(8,128)(2,1)} %constant.12.clone.pack_hbm, f32[40,2560]{1,0:T(8,128)} %coef_hbm.1, ...), custom_call_target="tpu_custom_call" | custom-call | tf_op jit(solution)/shard_map/whole/pallas_call | solution.py:583
  75.2 0.9 %copy.18 = bf16[4,6,16,1280]{3,2,1,0:T(8,128)(2,1)} copy(bf16[4,6,16,1280]{3,2,1,0:T(8,128)(2,1)S(1)} %whole.1) | data formatting | bytes 1966080

commit v6 on v5

--- a/solution.py
+++ b/solution.py
@@ -79,7 +79,7 @@
         waves_out[t, rows, :] = out.astype(BF)
         return 0
 
-    lax.fori_loop(0, 640 // step, block, 0)
+    lax.fori_loop(0, 640 // step, block, 0, unroll=True)
 
 
 def inverse_pack(pack, waves_out, send):
@@ -93,7 +93,7 @@
                 send[rows, :] = y[half * 128 : half * 128 + 128, side * 128 : side * 128 + 128]
         return 0
 
-    lax.fori_loop(0, 8, block, 0, unroll=4)
+    lax.fori_loop(0, 8, block, 0, unroll=8)
 
 
 def cos_sin(steps, count):
@@ -171,7 +171,7 @@
                         fields[u, rows, r * 128 : r * 128 + 128] = part[r * 48 + f * 16 : r * 48 + f * 16 + 16, :]
         return 0
 
-    lax.fori_loop(0, 4, pair, 0, unroll=2)
+    lax.fori_loop(0, 4, pair, 0, unroll=4)
 
 
 def grid_cycle(u, points, coef_row, table, fields, tend, analysed):
@@ -211,7 +211,7 @@
             send[rows, :] = y[:, h * 128 : h * 128 + 128]
         return 0
 
-    lax.fori_loop(0, 4, pair, 0, unroll=2)
+    lax.fori_loop(0, 4, pair, 0, unroll=4)
 
 
 def parity_parts(recv, packt, weight_col, parts):
@@ -231,7 +231,7 @@
             parts[f, rows, 128:256] = (weight * (north - south)).astype(BF)
         return 0
 
-    lax.fori_loop(0, 8, block, 0, unroll=4)
+    lax.fori_loop(0, 8, block, 0, unroll=8)
 
 
 def make_damp(wave, depth_col, damp):

time: 76.2 us -> 74.6 us (0.979)
  Pallas kernels: 75.2 us -> 73.6 us
    pallas_call x1, Pallas kernels: 75.2 us -> 73.6 us  [on_device(): pl.pallas_call(whole, out_shape=pltpu.VMEM((4, 6, 16, NT), BF), in_specs=...]
where the time goes in v6:
time: 74.6 us; the launch traced here: 74.5 us
  Pallas kernels  73.6 us (99%)
  local copies, waits for them, and re-layouts  0.95 us (1%)
    pallas_call x1, Pallas kernels, on_device(): pl.pallas_call(whole, out_shape=pltpu.VMEM((4, 6, 16, NT), BF), in_specs=...  73.6 us

profile of v6, /device:TPU:1, one launch (start us, length us, event | category | flops | bytes accessed | tf_op | source)
XLA Modules:
  0.0 74.5 jit_solution(14921084143502303570)
XLA Ops:
  0.0 73.6 %whole.1 = bf16[4,6,16,1280]{3,2,1,0:T(8,128)(2,1)S(1)} custom-call(s32[128]{0:T(128)} %lens_hbm.1, s32[128]{0:T(128)} %waves_hbm.1, s32[1280]{0:T(1024)} %cyc_hbm.1, bf16[384,1280]{1,0:T(8,128)(2,1)} %bitcast.3, bf16[4,640,1280]{2,1,0:T(8,128)(2,1)} %leg_hbm.1, bf16[256,240]{1,0:T(8,128)(2,1)} %constant.12.clone.pack_hbm, f32[40,2560]{1,0:T(8,128)} %coef_hbm.1, ...), custom_call_target="tpu_custom_call" | custom-call | tf_op jit(solution)/shard_map/whole/pallas_call | solution.py:583
  73.6 0.9 %copy.18 = bf16[4,6,16,1280]{3,2,1,0:T(8,128)(2,1)} copy(bf16[4,6,16,1280]{3,2,1,0:T(8,128)(2,1)S(1)} %whole.1) | data formatting | bytes 1966080
